TPU v7x, 128 devices: a whole 4x4x4 slice. The times are simulated.
128 devices in a mesh: col: 2 (over core), row: 64 (over z, y, x).
Axes of the slice: x: 4, y: 4, z: 4, core: 2. Of those that a mesh axis runs over, the one named last changes fastest.
Arguments:
- hyper_params: float32 [3], replicated
- w_in: float32 [1, 1024, 65536], P(None, 'row', 'col')
- x_in: bfloat16 [1, 1024, 1024], P(None, None, 'row')
- dy_in: bfloat16 [1, 1024, 65536], P(None, None, 'col')
- row_in: float32 [1, 1024], P(None, 'row')
- col_in: float32 [1, 65536], P(None, 'col')
- w_out: float32 [1, 65536, 1024], P(None, 'col', 'row')
- x_out: bfloat16 [1, 1024, 65536], P(None, None, 'col')
- dy_out: bfloat16 [1, 1024, 1024], P(None, None, 'row')
- row_out: float32 [1, 65536], P(None, 'col')
- col_out: float32 [1, 1024], P(None, 'row')
Outputs:
- output 1: float32 [1, 1024, 65536], P(None, 'row', 'col')
- output 2: float32 [1, 1024], P(None, 'row')
- output 3: float32 [1, 65536], P(None, 'col')
- output 4: float32 [1, 65536, 1024], P(None, 'col', 'row')
- output 5: float32 [1, 65536], P(None, 'col')
- output 6: float32 [1, 1024], P(None, 'row')
All inputs are finite; a program needn't handle non-finite values.
Results may differ from a plain program's by a relative error of at most 0.001.
Values are sent between devices in bfloat16 or wider.
A program may use at most 1 GiB of HBM per device.

v0:
```python
import jax
import jax.numpy as jnp
from jax import lax
from jax.sharding import PartitionSpec as P

EPS_ONE = 1e-30
EPS_TWO = 1e-3
BOTH_AXES = ('col', 'row')


def update_block(w_blk, x_blk, dy_blk, row_old, col_old, hyper_params, rows_axis, cols_axis, n_rows, n_cols):
    beta_two = hyper_params[0]
    rho_step = hyper_params[1]
    clip_max = hyper_params[2]
    n_total = float(n_rows * n_cols)
    grad_blk = lax.dot_general(x_blk, dy_blk, (((0,), (0,)), ((), ())), preferred_element_type=jnp.float32)
    sq_grad = grad_blk * grad_blk + EPS_ONE
    row_part = jnp.sum(sq_grad, axis=1)
    col_part = jnp.sum(sq_grad, axis=0)
    lead_col = (lax.axis_index(cols_axis) == 0).astype(jnp.float32)
    scalars = jnp.stack([jnp.sum(row_part), jnp.sum(w_blk * w_blk), lead_col * jnp.sum(row_old)])
    row_sum = lax.psum(row_part, cols_axis)
    col_sum = lax.psum(col_part, rows_axis)
    scalar_sum = lax.psum(scalars, BOTH_AXES)
    row_new = beta_two * row_old + (1.0 - beta_two) * (row_sum / n_cols)
    col_new = beta_two * col_old + (1.0 - beta_two) * (col_sum / n_rows)
    row_mean = beta_two * (scalar_sum[2] / n_rows) + (1.0 - beta_two) * (scalar_sum[0] / n_total)
    update = grad_blk * lax.rsqrt((row_new / row_mean)[:, None] * col_new[None, :])
    upd_sq = lax.psum(jnp.sum(update * update), BOTH_AXES)
    upd_rms = jnp.sqrt(upd_sq / n_total)
    w_rms = jnp.sqrt(scalar_sum[1] / n_total)
    step_size = rho_step * jnp.maximum(EPS_TWO, w_rms) / jnp.maximum(1.0, upd_rms / clip_max)
    return w_blk - step_size * update, row_new, col_new


def solution(mesh):
    n_col = mesh.shape['col']
    n_row = mesh.shape['row']
    tile_in = P(None, 'row', 'col')
    tile_out = P(None, 'col', 'row')
    lane_row = P(None, None, 'row')
    lane_col = P(None, None, 'col')
    vec_row = P(None, 'row')
    vec_col = P(None, 'col')

    def local_step(hyper_params, w_in, x_in, dy_in, row_in, col_in, w_out, x_out, dy_out, row_out, col_out):
        d_model = w_in.shape[1] * n_row
        d_hidden = w_in.shape[2] * n_col
        results = []
        for layer_idx in range(w_in.shape[0]):
            in_result = update_block(w_in[layer_idx], x_in[layer_idx], dy_in[layer_idx], row_in[layer_idx], col_in[layer_idx], hyper_params, 'row', 'col', d_model, d_hidden)
            out_result = update_block(w_out[layer_idx], x_out[layer_idx], dy_out[layer_idx], row_out[layer_idx], col_out[layer_idx], hyper_params, 'col', 'row', d_hidden, d_model)
            results.append(in_result + out_result)
        return tuple(jnp.stack([res_item[out_idx] for res_item in results]) for out_idx in range(6))

    return jax.shard_map(local_step, mesh=mesh, in_specs=(P(), tile_in, lane_row, lane_col, vec_row, vec_col, tile_out, lane_col, lane_row, vec_col, vec_row), out_specs=(tile_in, vec_row, vec_col, tile_out, vec_col, vec_row), check_vma=False)
```

profile of v0, /device:TPU:1, one launch (start us, length us, event | category | flops | bytes accessed | tf_op | source)
XLA Modules:
  0.0 274.3 jit_solution(7150685000777208344)
XLA Ops:
  7.2 0.0 copy-start
  7.2 0.0 copy-start.6
  7.2 0.0 all-reduce.6.cloned.1.call-start
  7.2 0.7 copy-done
  7.9 24.1 %fusion.9 = (f32[16]{0:T(128)S(1)}, f32[32768]{0:T(1024)}, f32[]{:T(128)}, f32[16,32768]{1,0:T(8,128)S(1)}) fusion(bf16[1,1024,32768]{2,1,0:T(8,128)(2,1)} %param.14, bf16[1,1024,16]{1,2,0:T(8,128)(2,1)S(1)} %copy-done), kind=kOutput, calls=%fused_computation.19 | convolution fusion | flops 1076330496 | bytes 69369920 | tf_op jit(solution)/shard_map/dot_general | solution.py:16
  32.1 0.0 copy-done.6
  32.1 25.5 %fusion.12 = (f32[32768]{0:T(1024)}, f32[16]{0:T(128)S(1)}, f32[]{:T(128)}, f32[32768,16]{0,1:T(8,128)}) fusion(bf16[1,1024,32768]{2,1,0:T(8,128)(2,1)} %param.18, bf16[1,1024,16]{1,2,0:T(8,128)(2,1)S(1)} %copy-done.6), kind=kOutput, calls=%fused_computation.22 | convolution fusion | flops 1076330496 | bytes 69369920 | tf_op jit(solution)/shard_map/dot_general | solution.py:16
  57.5 0.0 all-reduce.6.cloned.1.call-update
  57.6 0.0 copy-start.2
  57.6 0.0 copy-start.7
  57.6 0.0 copy-start.9
  57.6 0.0 copy-start.4
  57.6 0.0 copy-start.5
  57.6 0.0 copy-start.10
  57.6 3.0 %fusion.4 = f32[]{:T(128)} fusion(f32[1,32768,16]{1,2,0:T(8,128)} %param.17), kind=kLoop, calls=%fused_computation.6 | loop fusion | flops 1048575 | bytes 2097156 | tf_op jit(solution)/shard_map/reduce_sum | solution.py:21
  60.6 0.0 copy-done.2
  60.6 1.2 fusion.6
  61.8 0.0 copy-done.7
  61.8 0.6 fusion.17
  62.5 0.0 copy-done.9
  62.5 0.6 reduce_sum.110
  63.7 0.0 copy-done.4
  63.7 1.5 broadcast_multiply_fusion
  65.9 1.4 pad_maximum_fusion
  67.3 1.3 pad_maximum_fusion.1
  68.6 0.0 copy-done.5
  68.6 0.7 broadcast_multiply_fusion.1
  69.3 69.0 %all-reduce.1 = (f32[3]{0:T(128)S(1)}, f32[3]{0:T(128)S(1)}) all-reduce(f32[3]{0:T(128)S(1)} %pad_maximum_fusion, f32[3]{0:T(128)S(1)} %pad_maximum_fusion.1), channel_id=1, replica_groups=mesh['col'=2,'row'=64] {'col','row'}, use_global_device_ids=true, to_apply=%region_3.0 | all-reduce | flops 6 | bytes 48 | tf_op jit(solution)/shard_map/psum | solution.py:24
  138.4 0.6 fusion.18
  138.9 0.7 fusion.16
  146.0 2.7 all-reduce.3
  148.8 0.0 copy-done.10
  148.8 1.1 broadcast_divide_fusion.1
  149.9 0.0 copy-start.8
  149.9 37.8 %all-reduce.6.cloned.1.call-done = (f32[32768]{0:T(1024)}, f32[32768]{0:T(1024)}) async-done(((f32[32768]{0:T(1024)}, f32[32768]{0:T(1024)}), (f32[32768]{0:T(1024)}, f32[32768]{0:T(1024)})) %all-reduce.6.cloned.1.call-update) | async-done | bytes 262160 | tf_op jit(solution)/shard_map/psum | solution.py:23
  187.7 0.0 copy-start.1
  187.7 1.8 broadcast_divide_fusion
  189.6 0.0 copy-start.3
  189.6 1.4 multiply_reduce_fusion.1
  190.9 0.0 copy-done.1
  190.9 1.3 multiply_reduce_fusion
  192.8 64.6 %all-reduce = (f32[]{:T(128)}, f32[]{:T(128)}) all-reduce(f32[]{:T(128)} %multiply_reduce_fusion.1, f32[]{:T(128)} %multiply_reduce_fusion), channel_id=1, replica_groups=mesh['col'=2,'row'=64] {'col','row'}, use_global_device_ids=true, to_apply=%region_9.0 | all-reduce | flops 2 | bytes 16 | tf_op jit(solution)/shard_map/psum | solution.py:29
  260.2 0.0 copy-done.8
  260.2 4.0 %fusion.5 = f32[1,32768,16]{1,2,0:T(8,128)} fusion(f32[1,32768,16]{1,2,0:T(8,128)} %param.17, f32[32768,16]{0,1:T(8,128)} %get-tuple-element.36, f32[]{:T(128)S(6)} %div.79, f32[16]{0:T(128)S(1)} %get-tuple-element.37, f32[32768]{0:T(1024)S(1)} %get-tuple-element.20), kind=kLoop, calls=%fused_computation.7 | loop fusion | flops 2097152 | bytes 6422596 | tf_op jit(solution)/shard_map/stack | solution.py:54
  264.2 0.0 copy-done.3
  264.2 3.3 %fusion.7 = f32[1,16,32768]{2,1,0:T(8,128)} fusion(f32[1,16,32768]{2,1,0:T(8,128)} %param.12, f32[16,32768]{1,0:T(8,128)S(1)} %get-tuple-element.35, f32[]{:T(128)S(6)} %div.69, f32[32768]{0:T(1024)S(1)} %get-tuple-element.38, f32[16]{0:T(128)S(1)} %get-tuple-element.22), kind=kLoop, calls=%fused_computation.11 | loop fusion | flops 2097152 | bytes 6422596 | tf_op jit(solution)/shard_map/stack | solution.py:54
Async XLA Ops:
  7.2 0.8 copy-start
  7.2 24.9 %copy-start.6 = (bf16[1,1024,16]{1,2,0:T(8,128)(2,1)S(1)}, bf16[1,1024,16]{1,2,0:T(8,128)(2,1)}, u32[]{:S(2)}) copy-start(bf16[1,1024,16]{1,2,0:T(8,128)(2,1)} %param.19) | copy-start | bytes 98308
  7.2 180.6 %all-reduce.6.cloned.1.call-start = ((), (), s32[]{:S(2)}) async-start(), calls=%async_computation | async-start | bytes 524288 | tf_op jit(solution)/shard_map/psum | solution.py:23
  57.6 3.0 %copy-start.2 = (f32[1,16,32768]{2,1,0:T(8,128)S(1)}, f32[1,16,32768]{2,1,0:T(8,128)}, u32[]{:S(2)}) copy-start(f32[1,16,32768]{2,1,0:T(8,128)} %param.12) | copy-start | bytes 6291460
  57.6 4.2 %copy-start.7 = (f32[3]{0:T(128)S(1)}, f32[3]{0:T(128)}, u32[]{:S(2)}) copy-start(f32[3]{0:T(128)} %param.11) | copy-start | bytes 40
  57.6 4.9 %copy-start.9 = (f32[1,16]{1,0:T(1,128)S(1)}, f32[1,16]{1,0:T(1,128)}, u32[]{:S(2)}) copy-start(f32[1,16]{1,0:T(1,128)} %param.15) | copy-start | bytes 196
  57.6 6.1 %copy-start.4 = (f32[1,32768]{1,0:T(1,128)S(1)}, f32[1,32768]{1,0:T(1,128)}, u32[]{:S(2)}) copy-start(f32[1,32768]{1,0:T(1,128)} %param.20) | copy-start | bytes 393220
  57.6 11.0 %copy-start.5 = (f32[1,32768]{1,0:T(1,128)S(1)}, f32[1,32768]{1,0:T(1,128)}, u32[]{:S(2)}) copy-start(f32[1,32768]{1,0:T(1,128)} %param.16) | copy-start | bytes 393220
  57.6 91.1 %copy-start.10 = (f32[1,16]{1,0:T(1,128)S(1)}, f32[1,16]{1,0:T(1,128)}, u32[]{:S(2)}) copy-start(f32[1,16]{1,0:T(1,128)} %param.21) | copy-start | bytes 196
  149.9 110.3 %copy-start.8 = (f32[16]{0:T(128)}, f32[16]{0:T(128)S(1)}, u32[]{:S(2)}) copy-start(f32[16]{0:T(128)S(1)} %get-tuple-element.37) | copy-start | bytes 196
  187.7 3.2 %copy-start.1 = (f32[32768,16]{0,1:T(8,128)S(1)}, f32[32768,16]{0,1:T(8,128)}, u32[]{:S(2)}) copy-start(f32[32768,16]{0,1:T(8,128)} %get-tuple-element.36) | copy-start | bytes 6291460
  189.6 74.6 %copy-start.3 = (f32[32768]{0:T(1024)}, f32[32768]{0:T(1024)S(1)}, u32[]{:S(2)}) copy-start(f32[32768]{0:T(1024)S(1)} %get-tuple-element.38) | copy-start | bytes 393220
Sparse Core Ops, SparseCore 0:
  57.7 130.0 all-reduce.5
where the time goes:
time: 275 us; the launch traced here: 274 us
  blocking collectives  136 us (49%)
  matrix products  49.6 us (18%)
  waiting for transfers between devices  37.9 us (14%)
  between operations  25.3 us (9%)
  other arithmetic  22.6 us (8%)
    psum x1, blocking collectives, update_block(): scalar_sum = lax.psum(scalars, BOTH_AXES)  69 us
    psum x1, blocking collectives, update_block(): upd_sq = lax.psum(jnp.sum(update * update), BOTH_AXES)  64.6 us
    dot_general x2, matrix products, update_block(): lax.dot_general(x_blk, dy_blk, (((0,), (0,)), ((), ())), preferred_elemen...  49.6 us
    psum x1, waiting for transfers between devices, update_block(): col_sum = lax.psum(col_part, rows_axis)  37.8 us
    another operation x2, other arithmetic, local_step(): jnp.stack([res_item[out_idx] for res_item in results])  7.28 us
  transfers between devices with their start and end apart: 1, of which 1 were waited for; matrix products, arithmetic and copies ran while one was open for 5% of the time, Pallas kernels for 0%

commit v1 on v0

v1 whole, which is shorter than its diff:
```python
import functools

import jax
import jax.numpy as jnp
from jax import lax
from jax.experimental import pallas as pl
from jax.experimental.pallas import tpu as pltpu
from jax.sharding import PartitionSpec as P

EPS_ONE = 1e-30
EPS_TWO = 1e-3
MESH = pl.DeviceIdType.MESH
F32 = jnp.float32

SHARE = ((0, 1, 3, 4, 12, 16, 48, 5), (0, 1, 3, 4, 12, 16, 48, 60))
CODE = (0, 14, 33, 55, 24, 22, 57, 47)
PARTNERS = tuple(sorted({m for lst in SHARE for m in lst[1:]} | set(CODE[1:])))
N_BLOCK = 8
CHUNK = 1024
SCALE = 2.0 ** -20


def digit_xor(v, m):
    if m == 0:
        return v
    if m == 1:
        return v + 1 - 2 * (v % 2)
    if m == 2:
        return (v + 2) % 4
    return 3 - v


def fold(x):
    acc = x[:, 0:128]
    for i in range(1, x.shape[1] // 128):
        acc = acc + x[:, i * 128:(i + 1) * 128]
    return acc


def stats_kernel(dims, hyper, a0, a1, so0, so1, bo0, bo1, b0, b1, w0, w1,
                 g0, g1, c0, c1, r_out, s_out,
                 a_all, b_buf, gs, w_buf, so_buf, bo_buf, ar_buf, cnew, rs_own, rs_in, rs_core, rp_all,
                 sc_buf, sh_buf, k_buf,
                 b_sem, w_sem, in_sem, own_sem,
                 a_ss, a_rs, g_ss, g_rs, rs_ss, rs_rs, rp_ss, rp_rs, c_ss, c_rs,
                 ar_ss, ar_rs, sc_ss, sc_rs, sh_ss, sh_rs, k_ss, k_rs):
    tile, width, block, n_small, n_big = dims
    n_chunk = block // CHUNK
    col = lax.axis_index('col')
    row = lax.axis_index('row')
    x, y, z = row % 4, (row // 4) % 4, row // 16
    bx, by, bz = x // 2, y // 2, z // 2
    ax, ay, az = (x + bx) % 2, (y + by) % 2, (z + bz) % 2
    syn = (ax + by + az) % 2 + 2 * ((bx + ay + by) % 2) + 4 * ((ay + az + bz) % 2)
    rank = bx + 2 * bz + 4 * ay
    base = pl.multiple_of(syn * block, block)

    def peer(mask):
        return (col, digit_xor(z, mask // 16) * 16 + digit_xor(y, (mask // 4) % 4) * 4 + digit_xor(x, mask % 4))

    core = (1 - col, row)
    a_in, so_in, bo_in, b_in, w_in = (a0, a1), (so0, so1), (bo0, bo1), (b0, b1), (w0, w1)
    g_out, c_out = (g0, g1), (c0, c1)

    def rcopy(src, dst, ss, rs, dev):
        return pltpu.make_async_remote_copy(src_ref=src, dst_ref=dst, send_sem=ss, recv_sem=rs, device_id=dev, device_id_type=MESH)

    barrier = pltpu.get_barrier_semaphore()
    for mask in PARTNERS:
        pl.semaphore_signal(barrier, inc=1, device_id=peer(mask), device_id_type=MESH)
    pl.semaphore_signal(barrier, inc=1, device_id=core, device_id_type=MESH)

    a_load = [pltpu.make_async_copy(a_in[m], a_all.at[m, 0:tile], in_sem.at[m]) for m in range(2)]
    for cp in a_load:
        cp.start()

    def b_load(m, c):
        return pltpu.make_async_copy(b_in[m].at[:, pl.ds(pl.multiple_of(base + c * CHUNK, CHUNK), CHUNK)], b_buf.at[m, c], b_sem.at[m, c])

    for c in range(n_chunk):
        for m in range(2):
            b_load(m, c).start()
    misc = []
    for m in range(2):
        misc.append(pltpu.make_async_copy(so_in[m], so_buf.at[m], in_sem.at[2 + m]))
        misc.append(pltpu.make_async_copy(bo_in[m], bo_buf.at[m], in_sem.at[4 + m]))
        misc.append(pltpu.make_async_copy(w_in[m], w_buf.at[m], w_sem.at[m]))
    for cp in misc:
        cp.start()

    for cp in a_load:
        cp.wait()
    pl.semaphore_wait(barrier, len(PARTNERS) + 1)

    def a_copy(m, j):
        return rcopy(a_all.at[m, 0:tile], a_all.at[m, j * tile:(j + 1) * tile], a_ss.at[m, j], a_rs.at[m, j], peer(SHARE[m][j]))

    for m in range(2):
        for j in range(1, N_BLOCK):
            a_copy(m, j).start()

    def g_copy(m, j, lo, size):
        return rcopy(gs.at[m, j * tile:(j + 1) * tile, lo:lo + size], g_out[m].at[:, pl.ds(pl.multiple_of(base + lo, CHUNK), size)],
                     g_ss.at[m, j], g_rs.at[m, j], peer(SHARE[m][j]))

    def g_own(m, lo, size):
        return pltpu.make_async_copy(gs.at[m, 0:tile, lo:lo + size], g_out[m].at[:, pl.ds(pl.multiple_of(base + lo, CHUNK), size)], own_sem.at[m])

    def send_g(m, c):
        for j in range(1, N_BLOCK):
            g_copy(m, j, c * CHUNK, CHUNK).start()

    def compute(m, c):
        b_load(m, c).wait()
        g = jnp.dot(a_all[m], b_buf[m, c], preferred_element_type=F32)
        gs[m, :, c * CHUNK:(c + 1) * CHUNK] = g
        sq = g * g
        ar_buf[rank, :, m * block + c * CHUNK:m * block + (c + 1) * CHUNK] = jnp.sum(sq, axis=0, keepdims=True)
        part = fold(sq)
        if c == 0:
            rs_own[m] = part
        else:
            rs_own[m] = rs_own[m] + part

    for m in range(2):
        for j in range(1, N_BLOCK):
            a_copy(m, j).wait_recv()
    for c in range(n_chunk):
        for m in range(2):
            compute(m, c)
        if c == 0:
            send_g(0, 0)

    def rs_copy(m, j):
        return rcopy(rs_own.at[m, j * tile:(j + 1) * tile], rs_in.at[m, j * tile:(j + 1) * tile], rs_ss.at[m, j], rs_rs.at[m, j], peer(SHARE[m][j]))

    def ar_copy(j):
        return rcopy(ar_buf.at[rank], ar_buf.at[rank], ar_ss.at[j], ar_rs.at[j], peer(CODE[j]))

    for m in range(2):
        for j in range(1, N_BLOCK):
            rs_copy(m, j).start()
    for j in range(1, N_BLOCK):
        ar_copy(j).start()
    for m in range(2):
        g_own(m, 0, block).start()
    send_g(1, 0)

    w_load = [misc[2], misc[5]]
    for m in range(2):
        w_load[m].wait()

        def w_step(i, acc):
            blk = w_buf[m, :, pl.ds(pl.multiple_of(i * 1024, 1024), 1024)]
            return acc + fold(blk * blk)

        w_acc = lax.fori_loop(0, width // 1024, w_step, jnp.zeros((tile, 128), F32))
        sc_buf[0, 4 * m + 2:4 * m + 3, :] = jnp.sum(w_acc, axis=0, keepdims=True)
    for i in (0, 1, 3, 4):
        misc[i].wait()
    old0 = jnp.sum(so_buf[0], axis=1, keepdims=True) * (0.5 / 128)
    old1 = jnp.sum(bo_buf[1], axis=1, keepdims=True) * (1.0 / (64 * 128))
    sc_buf[0, 3:4, :] = jnp.broadcast_to(old0, (1, 128))
    sc_buf[0, 7:8, :] = jnp.broadcast_to(old1, (1, 128))
    for m in range(2):
        sc_buf[0, 4 * m + 1:4 * m + 2, :] = jnp.sum(rs_own[m], axis=0, keepdims=True)

    for m in range(2):
        for j in range(1, N_BLOCK):
            rs_copy(m, j).wait_recv()
        total = rs_own[m, 0:tile]
        for j in range(1, N_BLOCK):
            total = total + rs_in[m, j * tile:(j + 1) * tile]
        rs_core[0, m] = total
    core_rows = rcopy(rs_core.at[0], rs_core.at[1], k_ss.at[0], k_rs.at[0], core)
    core_rows.start()
    send_g(0, 1)
    core_rows.wait_recv()
    beta_two = hyper[0]
    rho_step = hyper[1]
    clip_max = hyper[2]
    eye = lax.broadcasted_iota(jnp.int32, (tile, tile), 0) == lax.broadcasted_iota(jnp.int32, (tile, tile), 1)
    for m in range(2):
        total = jnp.sum(rs_core[0, m] + rs_core[1, m], axis=1, keepdims=True)
        old = jnp.sum(jnp.where(eye, jnp.broadcast_to(so_buf[m], (tile, tile)), 0.0), axis=1, keepdims=True)
        new = beta_two * old + (1.0 - beta_two) * (total * (1.0 / n_big) + EPS_ONE)
        rp_all[m, 0:tile] = jnp.broadcast_to(new, (tile, 128))
        r_out[m] = jnp.broadcast_to(new, (tile, 128))

    def rp_copy(m, j):
        return rcopy(rp_all.at[m, 0:tile], rp_all.at[m, j * tile:(j + 1) * tile], rp_ss.at[m, j], rp_rs.at[m, j], peer(SHARE[m][j]))

    for m in range(2):
        for j in range(1, N_BLOCK):
            rp_copy(m, j).start()

    for j in range(1, N_BLOCK):
        ar_copy(j).wait()
    for m in range(2):
        lanes = slice(m * block, (m + 1) * block)
        total = ar_buf[0, :, lanes]
        for j in range(1, N_BLOCK):
            total = total + ar_buf[j, :, lanes]
        old = bo_buf[m, :, pl.ds(base, block)]
        cnew[m] = beta_two * old + (1.0 - beta_two) * (total * (1.0 / n_small) + EPS_ONE)

    def c_copy(m, j):
        return rcopy(cnew.at[m], c_out[m].at[:, pl.ds(base, block)], c_ss.at[m, j], c_rs.at[m, j], peer(SHARE[m][j]))

    c_own = [pltpu.make_async_copy(cnew.at[m], c_out[m].at[:, pl.ds(base, block)], in_sem.at[6 + m]) for m in range(2)]
    for m in range(2):
        for j in range(1, N_BLOCK):
            c_copy(m, j).start()
        c_own[m].start()

    for m in range(2):
        def u_step(i, acc):
            lanes = pl.ds(pl.multiple_of(i * 512, 512), 512)
            blk = gs[m, :, lanes]
            return acc + fold(blk * blk * (1.0 / cnew[m, :, lanes]))

        u_acc = lax.fori_loop(0, block // 512, u_step, jnp.zeros((N_BLOCK * tile, 128), F32))
        for j in range(1, N_BLOCK):
            rp_copy(m, j).wait()
        sc_buf[0, 4 * m:4 * m + 1, :] = jnp.sum(u_acc * SCALE / rp_all[m], axis=0, keepdims=True)

    def sc_copy(j):
        return rcopy(sc_buf.at[0], sc_buf.at[j], sc_ss.at[j], sc_rs.at[j], peer(CODE[j]))

    def sh_copy(j):
        return rcopy(sh_buf.at[0], sh_buf.at[j], sh_ss.at[j], sh_rs.at[j], peer(SHARE[0][j]))

    for j in range(1, N_BLOCK):
        sc_copy(j).start()
    send_g(1, 1)
    send_g(0, 2)
    for j in range(1, N_BLOCK):
        sc_copy(j).wait()
    total = sc_buf[0]
    for j in range(1, N_BLOCK):
        total = total + sc_buf[j]
    sh_buf[0] = total
    for j in range(1, N_BLOCK):
        sh_copy(j).start()
    send_g(1, 2)
    send_g(0, 3)
    send_g(1, 3)
    for j in range(1, N_BLOCK):
        sh_copy(j).wait()
    total = sh_buf[0]
    for j in range(1, N_BLOCK):
        total = total + sh_buf[j]
    k_buf[0] = total
    core_sum = rcopy(k_buf.at[0], k_buf.at[1], k_ss.at[1], k_rs.at[1], core)
    core_sum.start()
    core_sum.wait()
    sums = jnp.broadcast_to(jnp.sum(k_buf[0] + k_buf[1], axis=1, keepdims=True), (8, 128))
    n_total = float(n_small) * float(n_big)
    for m, n_rows in ((0, n_small), (1, n_big)):
        u_sum, g_sum, w_sum, r_sum = (sums[4 * m + i:4 * m + i + 1] for i in range(4))
        row_mean = beta_two * (r_sum * (1.0 / n_rows)) + (1.0 - beta_two) * (g_sum * (1.0 / n_total) + EPS_ONE)
        upd_rms = jnp.sqrt(u_sum * row_mean * (1.0 / (n_total * SCALE)))
        w_rms = jnp.sqrt(w_sum * (1.0 / n_total))
        step_size = rho_step * jnp.maximum(EPS_TWO, w_rms) / jnp.maximum(1.0, upd_rms / clip_max)
        s_out[m:m + 1, :] = step_size * jnp.sqrt(row_mean)

    core_rows.wait_send()
    for m in range(2):
        g_own(m, 0, block).wait()
        c_own[m].wait()
        for j in range(1, N_BLOCK):
            a_copy(m, j).wait_send()
            rs_copy(m, j).wait_send()
            c_copy(m, j).wait()
            g_copy(m, j, 0, block).wait()


def apply_kernel(g0, g1, w0, w1, c0, c1, r_new, scal, w0_new, w1_new, c0_new, c1_new, r0_new, r1_new):
    tile = w0.shape[0]
    for m, (g, w, c, w_new, c_new) in enumerate(((g0, w0, c0, w0_new, c0_new), (g1, w1, c1, w1_new, c1_new))):
        row_scale = scal[m:m + 1, 0:1] * lax.rsqrt(r_new[m, :, 0:1])
        w_new[...] = w[...] - (g[...] * lax.rsqrt(c[...])) * row_scale
        c_new[...] = c[...]

    @pl.when(pl.program_id(0) == 0)
    def _():
        eye = lax.broadcasted_iota(jnp.int32, (tile, tile), 0) == lax.broadcasted_iota(jnp.int32, (tile, tile), 1)
        for m, r_row in ((0, r0_new), (1, r1_new)):
            r_row[...] = jnp.sum(jnp.where(eye, r_new[m, :, 0:tile], 0.0), axis=0, keepdims=True)


def solution(mesh):
    tile_in = P(None, 'row', 'col')
    tile_out = P(None, 'col', 'row')
    lane_row = P(None, None, 'row')
    lane_col = P(None, None, 'col')
    vec_row = P(None, 'row')
    vec_col = P(None, 'col')
    n_row = mesh.shape['row']
    n_col = mesh.shape['col']

    def local_step(hyper_params, w_in, x_in, dy_in, row_in, col_in, w_out, x_out, dy_out, row_out, col_out):
        tile, width = w_in.shape[1], w_in.shape[2]
        tokens = x_in.shape[1]
        block = width // N_BLOCK
        n_chunk = block // CHUNK
        dims = (tile, width, block, tile * n_row, width * n_col)
        rows = N_BLOCK * tile
        w0 = w_in[0]
        w1 = jnp.transpose(w_out[0])
        a0 = jnp.transpose(x_in[0])
        a1 = jnp.transpose(dy_out[0])
        dma = pltpu.SemaphoreType.DMA
        any_spec = pl.BlockSpec(memory_space=pl.ANY)
        hbm_spec = pl.BlockSpec(memory_space=pltpu.HBM)
        vmem_spec = pl.BlockSpec(memory_space=pltpu.VMEM)
        g0, g1, c0, c1, r_new, scal = pl.pallas_call(
            functools.partial(stats_kernel, dims),
            out_shape=(
                jax.ShapeDtypeStruct((tile, width), F32),
                jax.ShapeDtypeStruct((tile, width), F32),
                jax.ShapeDtypeStruct((1, width), F32),
                jax.ShapeDtypeStruct((1, width), F32),
                jax.ShapeDtypeStruct((2, tile, 128), F32),
                jax.ShapeDtypeStruct((8, 128), F32),
            ),
            in_specs=[pl.BlockSpec(memory_space=pltpu.SMEM)] + [any_spec] * 10,
            out_specs=(hbm_spec, hbm_spec, hbm_spec, hbm_spec, vmem_spec, vmem_spec),
            scratch_shapes=[
                pltpu.VMEM((2, rows, tokens), jnp.bfloat16),
                pltpu.VMEM((2, n_chunk, tokens, CHUNK), jnp.bfloat16),
                pltpu.VMEM((2, rows, block), F32),
                pltpu.VMEM((2, tile, width), F32),
                pltpu.VMEM((2, 1, tile), F32),
                pltpu.VMEM((2, 1, width), F32),
                pltpu.VMEM((N_BLOCK, 1, 2 * block), F32),
                pltpu.VMEM((2, 1, block), F32),
                pltpu.VMEM((2, rows, 128), F32),
                pltpu.VMEM((2, rows, 128), F32),
                pltpu.VMEM((2, 2, tile, 128), F32),
                pltpu.VMEM((2, rows, 128), F32),
                pltpu.VMEM((N_BLOCK, 8, 128), F32),
                pltpu.VMEM((N_BLOCK, 8, 128), F32),
                pltpu.VMEM((2, 8, 128), F32),
                dma((2, n_chunk)), dma((2,)), dma((8,)), dma((2,)),
                dma((2, 8)), dma((2, 8)), dma((2, 8)), dma((2, 8)), dma((2, 8)), dma((2, 8)),
                dma((2, 8)), dma((2, 8)), dma((2, 8)), dma((2, 8)),
                dma((8,)), dma((8,)), dma((8,)), dma((8,)), dma((8,)), dma((8,)), dma((2,)), dma((2,)),
            ],
            compiler_params=pltpu.CompilerParams(collective_id=0, has_side_effects=True, vmem_limit_bytes=48 * 1024 * 1024),
            name='stats',
        )(hyper_params, a0, a1, row_in, col_out, col_in, row_out, dy_in[0], x_out[0], w0, w1)

        step = 4096
        tile_spec = pl.BlockSpec((tile, step), lambda i: (0, i))
        vec_spec = pl.BlockSpec((1, step), lambda i: (0, i))
        w0_new, w1_new, c0_new, c1_new, r0_new, r1_new = pl.pallas_call(
            apply_kernel,
            grid=(width // step,),
            out_shape=(
                jax.ShapeDtypeStruct((tile, width), F32),
                jax.ShapeDtypeStruct((tile, width), F32),
                jax.ShapeDtypeStruct((1, width), F32),
                jax.ShapeDtypeStruct((1, width), F32),
                jax.ShapeDtypeStruct((1, tile), F32),
                jax.ShapeDtypeStruct((1, tile), F32),
            ),
            in_specs=[tile_spec, tile_spec, tile_spec, tile_spec, vec_spec, vec_spec,
                      pl.BlockSpec((2, tile, 128), lambda i: (0, 0, 0)), pl.BlockSpec((8, 128), lambda i: (0, 0))],
            out_specs=(tile_spec, tile_spec, vec_spec, vec_spec,
                       pl.BlockSpec((1, tile), lambda i: (0, 0)), pl.BlockSpec((1, tile), lambda i: (0, 0))),
            name='apply',
        )(g0, g1, w0, w1, c0, c1, r_new, scal)
        return w0_new[None], r0_new, c0_new, jnp.transpose(w1_new)[None], c1_new, r1_new

    return jax.shard_map(local_step, mesh=mesh, in_specs=(P(), tile_in, lane_row, lane_col, vec_row, vec_col, tile_out, lane_col, lane_row, vec_col, vec_row), out_specs=(tile_in, vec_row, vec_col, tile_out, vec_col, vec_row), check_vma=False)
```

time: 275 us -> 65.6 us (0.24)
  the two profiles are of different devices: /device:TPU:1 before, /device:TPU:0 now
where the time goes in v1:
time: 65.6 us; the launch traced here: 65.1 us
  Pallas kernels  54 us (82%)
  local copies, waits for them, and re-layouts  10.4 us (16%)
  between operations  0.67 us (1%)
    pallas_call x1, Pallas kernels, local_step(): pl.pallas_call(functools.partial(stats_kernel, dims), out_shape=(jax.Shap...  46 us
    unnamed x26, local copies, waits for them, and re-layouts  10.4 us
    pallas_call x1, Pallas kernels, local_step(): pl.pallas_call(apply_kernel, grid=(width // step,), out_shape=(jax.ShapeD...  7.99 us

profile of v1, /device:TPU:0, one launch (start us, length us, event | category | flops | bytes accessed | tf_op | source)
XLA Modules:
  0.0 65.1 jit_solution(6668196174699763345)
XLA Ops:
  0.6 0.0 copy-start.2
  0.6 0.9 %copy-done.2 = f32[1,32768]{1,0:T(1,128)S(1)} copy-done((f32[1,32768]{1,0:T(1,128)S(1)}, f32[1,32768]{1,0:T(1,128)}, u32[]{:S(2)}) %copy-start.2) | copy-done | bytes 131096
  1.5 0.0 copy-start.3
  1.5 0.9 %copy-done.3 = f32[1,32768]{1,0:T(1,128)S(1)} copy-done((f32[1,32768]{1,0:T(1,128)S(1)}, f32[1,32768]{1,0:T(1,128)}, u32[]{:S(2)}) %copy-start.3) | copy-done | bytes 131096
  2.4 0.0 copy-start.6
  2.4 0.8 %copy-done.6 = bf16[1,1024,16]{1,2,0:T(8,128)(2,1)S(1)} copy-done((bf16[1,1024,16]{1,2,0:T(8,128)(2,1)S(1)}, bf16[1,1024,16]{1,2,0:T(8,128)(2,1)}, u32[]{:S(2)}) %copy-start.6) | copy-done | bytes 32792
  3.2 0.0 copy-start.7
  3.2 0.8 %copy-done.7 = bf16[1,1024,16]{1,2,0:T(8,128)(2,1)S(1)} copy-done((bf16[1,1024,16]{1,2,0:T(8,128)(2,1)S(1)}, bf16[1,1024,16]{1,2,0:T(8,128)(2,1)}, u32[]{:S(2)}) %copy-start.7) | copy-done | bytes 32792
  4.0 0.0 copy-start.10
  4.0 0.7 %copy-done.10 = f32[3]{0:T(128)S(1)} copy-done((f32[3]{0:T(128)S(1)}, f32[3]{0:T(128)}, u32[]{:S(2)}) %copy-start.10) | copy-done | bytes 36
  4.6 0.0 copy-start.11
  4.6 0.7 %copy-done.11 = f32[1,16]{1,0:T(1,128)S(1)} copy-done((f32[1,16]{1,0:T(1,128)S(1)}, f32[1,16]{1,0:T(1,128)}, u32[]{:S(2)}) %copy-start.11) | copy-done | bytes 88
  5.3 0.0 copy-start.12
  5.3 0.7 %copy-done.12 = f32[1,16]{1,0:T(1,128)S(1)} copy-done((f32[1,16]{1,0:T(1,128)S(1)}, f32[1,16]{1,0:T(1,128)}, u32[]{:S(2)}) %copy-start.12) | copy-done | bytes 88
  5.9 46.0 %stats.1 = (f32[16,32768]{1,0:T(8,128)S(1)}, f32[16,32768]{1,0:T(8,128)S(1)}, f32[1,32768]{1,0:T(1,128)S(1)}, f32[1,32768]{1,0:T(1,128)S(1)}, f32[2,16,128]{2,1,0:T(8,128)S(1)}, /*index=5*/f32[8,128]{1,0:T(8,128)S(1)}) custom-call(f32[3]{0:T(128)S(1)} %copy-done.10, bf16[16,1024]{1,0:T(8,128)(2,1)S(1)} %bitcast.16, bf16[16,1024]{1,0:T(8,128)(2,1)S(1)} %bitcast.17, ...), custom_call_target="tpu_custom_call" | custom-call | tf_op jit(solution)/shard_map/stats/pallas_call | solution.py:317
  52.0 0.0 copy-start
  52.0 1.3 %copy-done = f32[16,32768]{1,0:T(8,128)} copy-done((f32[16,32768]{1,0:T(8,128)}, f32[16,32768]{1,0:T(8,128)S(1)}, u32[]{:S(2)}) %copy-start) | copy-done | bytes 2097176
  53.3 0.0 copy-start.1
  53.3 1.3 %copy-done.1 = f32[16,32768]{1,0:T(8,128)} copy-done((f32[16,32768]{1,0:T(8,128)}, f32[16,32768]{1,0:T(8,128)S(1)}, u32[]{:S(2)}) %copy-start.1) | copy-done | bytes 2097176
  54.6 0.0 copy-start.4
  54.6 0.7 %copy-done.4 = f32[1,32768]{1,0:T(1,128)} copy-done((f32[1,32768]{1,0:T(1,128)}, f32[1,32768]{1,0:T(1,128)S(1)}, u32[]{:S(2)}) %copy-start.4) | copy-done | bytes 131096
  55.3 0.0 copy-start.5
  55.3 0.7 %copy-done.5 = f32[1,32768]{1,0:T(1,128)} copy-done((f32[1,32768]{1,0:T(1,128)}, f32[1,32768]{1,0:T(1,128)S(1)}, u32[]{:S(2)}) %copy-start.5) | copy-done | bytes 131096
  56.0 0.0 copy-start.8
  56.0 0.6 copy-done.8
  56.6 0.0 copy-start.9
  56.6 0.6 copy-done.9
  57.1 8.0 %apply.1 = (f32[16,32768]{1,0:T(8,128)}, f32[16,32768]{1,0:T(8,128)}, f32[1,32768]{1,0:T(1,128)}, f32[1,32768]{1,0:T(1,128)}, f32[1,16]{1,0:T(1,128)}, /*index=5*/f32[1,16]{1,0:T(1,128)}) custom-call(f32[16,32768]{1,0:T(8,128)} %copy-done, f32[16,32768]{1,0:T(8,128)} %copy-done.1, f32[16,32768]{1,0:T(8,128)} %bitcast.19, f32[16,32768]{1,0:T(8,128)} %bitcast.21, ...), custom_call_target="tpu_custom_call" | custom-call | tf_op jit(solution)/shard_map/apply/pallas_call | solution.py:357
Async XLA Ops:
  0.6 0.9 %copy-start.2 = (f32[1,32768]{1,0:T(1,128)S(1)}, f32[1,32768]{1,0:T(1,128)}, u32[]{:S(2)}) copy-start(f32[1,32768]{1,0:T(1,128)} %bo0.1) | copy-start | bytes 393220
  1.5 0.9 %copy-start.3 = (f32[1,32768]{1,0:T(1,128)S(1)}, f32[1,32768]{1,0:T(1,128)}, u32[]{:S(2)}) copy-start(f32[1,32768]{1,0:T(1,128)} %bo1.1) | copy-start | bytes 393220
  2.4 0.8 %copy-start.6 = (bf16[1,1024,16]{1,2,0:T(8,128)(2,1)S(1)}, bf16[1,1024,16]{1,2,0:T(8,128)(2,1)}, u32[]{:S(2)}) copy-start(bf16[1,1024,16]{1,2,0:T(8,128)(2,1)} %param.13) | copy-start | bytes 98308
  3.2 0.8 %copy-start.7 = (bf16[1,1024,16]{1,2,0:T(8,128)(2,1)S(1)}, bf16[1,1024,16]{1,2,0:T(8,128)(2,1)}, u32[]{:S(2)}) copy-start(bf16[1,1024,16]{1,2,0:T(8,128)(2,1)} %param.19) | copy-start | bytes 98308
  4.0 0.7 %copy-start.10 = (f32[3]{0:T(128)S(1)}, f32[3]{0:T(128)}, u32[]{:S(2)}) copy-start(f32[3]{0:T(128)} %hyper.1) | copy-start | bytes 40
  4.6 0.7 %copy-start.11 = (f32[1,16]{1,0:T(1,128)S(1)}, f32[1,16]{1,0:T(1,128)}, u32[]{:S(2)}) copy-start(f32[1,16]{1,0:T(1,128)} %so0.1) | copy-start | bytes 196
  5.3 0.7 %copy-start.12 = (f32[1,16]{1,0:T(1,128)S(1)}, f32[1,16]{1,0:T(1,128)}, u32[]{:S(2)}) copy-start(f32[1,16]{1,0:T(1,128)} %so1.1) | copy-start | bytes 196
  52.0 1.3 %copy-start = (f32[16,32768]{1,0:T(8,128)}, f32[16,32768]{1,0:T(8,128)S(1)}, u32[]{:S(2)}) copy-start(f32[16,32768]{1,0:T(8,128)S(1)} %get-tuple-element.18.g0) | copy-start | bytes 6291460
  53.3 1.3 %copy-start.1 = (f32[16,32768]{1,0:T(8,128)}, f32[16,32768]{1,0:T(8,128)S(1)}, u32[]{:S(2)}) copy-start(f32[16,32768]{1,0:T(8,128)S(1)} %get-tuple-element.19.g1) | copy-start | bytes 6291460
  54.6 0.7 %copy-start.4 = (f32[1,32768]{1,0:T(1,128)}, f32[1,32768]{1,0:T(1,128)S(1)}, u32[]{:S(2)}) copy-start(f32[1,32768]{1,0:T(1,128)S(1)} %get-tuple-element.20.c0) | copy-start | bytes 393220
  55.3 0.7 %copy-start.5 = (f32[1,32768]{1,0:T(1,128)}, f32[1,32768]{1,0:T(1,128)S(1)}, u32[]{:S(2)}) copy-start(f32[1,32768]{1,0:T(1,128)S(1)} %get-tuple-element.21.c1) | copy-start | bytes 393220
  56.0 0.6 copy-start.8
  56.6 0.6 copy-start.9

commit v2 on v0

v2 whole, which is shorter than its diff:
```python
import functools

import jax
import jax.numpy as jnp
from jax import lax
from jax.experimental import pallas as pl
from jax.experimental.pallas import tpu as pltpu
from jax.sharding import PartitionSpec as P

EPS_ONE = 1e-30
EPS_TWO = 1e-3
MESH = pl.DeviceIdType.MESH
F32 = jnp.float32

SHARE = ((0, 1, 3, 4, 12, 16, 48, 5), (0, 1, 3, 4, 12, 16, 48, 60))
CODE = (0, 14, 33, 55, 24, 22, 57, 47)
PARTNERS = tuple(sorted({m for lst in SHARE for m in lst[1:]} | set(CODE[1:])))
FAR_PARTNERS = tuple(sorted({m for lst in SHARE for m in lst}))
N_BLOCK = 8
CHUNK = 1024
SCALE = 2.0 ** -20


def digit_xor(v, m):
    if m == 0:
        return v
    if m == 1:
        return v + 1 - 2 * (v % 2)
    if m == 2:
        return (v + 2) % 4
    return 3 - v


def fold(x):
    acc = x[:, 0:128]
    for i in range(1, x.shape[1] // 128):
        acc = acc + x[:, i * 128:(i + 1) * 128]
    return acc


def stats_kernel(dims, hyper, a0, a1, so0, so1, bo0, bo1, b0, b1, w0, w1,
                 g0, g1, c0, c1, wv0, wv1, r_out, s_out,
                 a_all, b_buf, b_far, gs, so_buf, bo_buf, ar_buf, cnew, rs_own, rs_in, rs_far, rp_all,
                 sc_buf, sh_buf, sf_buf,
                 b_sem, w_sem, in_sem, own_sem,
                 a_ss, a_rs, g_ss, g_rs, rs_ss, rs_rs, rf_ss, rf_rs, rp_ss, rp_rs, c_ss, c_rs,
                 ar_ss, ar_rs, sc_ss, sc_rs, sh_ss, sh_rs, sf_ss, sf_rs):
    tile, width, block, n_small, n_big = dims
    n_chunk = block // CHUNK
    col = lax.axis_index('col')
    row = lax.axis_index('row')
    x, y, z = row % 4, (row // 4) % 4, row // 16
    bx, by, bz = x // 2, y // 2, z // 2
    ax, ay, az = (x + bx) % 2, (y + by) % 2, (z + bz) % 2
    syn = (ax + by + az) % 2 + 2 * ((bx + ay + by) % 2) + 4 * ((ay + az + bz) % 2)
    rank = bx + 2 * bz + 4 * ay
    base = pl.multiple_of(syn * block, block)
    base_far = pl.multiple_of((N_BLOCK - 1 - syn) * block, block)
    peers = range(1, N_BLOCK)
    links = range(1, N_BLOCK - 1)

    def peer_row(mask):
        return digit_xor(z, mask // 16) * 16 + digit_xor(y, (mask // 4) % 4) * 4 + digit_xor(x, mask % 4)

    def near(mask):
        return (col, peer_row(mask))

    def far(mask):
        return (1 - col, peer_row(mask))

    a_in, so_in, bo_in, b_in, w_in = (a0, a1), (so0, so1), (bo0, bo1), (b0, b1), (w0, w1)
    g_out, c_out, wv = (g0, g1), (c0, c1), (wv0, wv1)

    def rcopy(src, dst, ss, rs, dev):
        return pltpu.make_async_remote_copy(src_ref=src, dst_ref=dst, send_sem=ss, recv_sem=rs, device_id=dev, device_id_type=MESH)

    barrier = pltpu.get_barrier_semaphore()
    for mask in PARTNERS:
        pl.semaphore_signal(barrier, inc=1, device_id=near(mask), device_id_type=MESH)
    for mask in FAR_PARTNERS:
        pl.semaphore_signal(barrier, inc=1, device_id=far(mask), device_id_type=MESH)

    a_load = [pltpu.make_async_copy(a_in[m], a_all.at[m, 0:tile], in_sem.at[m]) for m in range(2)]
    for cp in a_load:
        cp.start()

    def b_load(m, c):
        return pltpu.make_async_copy(b_in[m].at[:, pl.ds(pl.multiple_of(base + c * CHUNK, CHUNK), CHUNK)],
                                     b_buf.at[m, :, c * CHUNK:(c + 1) * CHUNK], b_sem.at[m, c])

    def b_far_load(m):
        return pltpu.make_async_copy(b_in[m].at[:, pl.ds(base_far, block)], b_far.at[m], b_sem.at[m, n_chunk])

    so_load = [pltpu.make_async_copy(so_in[m], so_buf.at[m], in_sem.at[2 + m]) for m in range(2)]
    bo_load = [pltpu.make_async_copy(bo_in[m], bo_buf.at[m], in_sem.at[4 + m]) for m in range(2)]
    w_load = [pltpu.make_async_copy(w_in[m], wv[m], w_sem.at[m]) for m in range(2)]
    for cp in a_load:
        cp.wait()
    for c in range(n_chunk):
        b_load(0, c).start()
    with jax.named_scope('p00_barrier'):
        pl.semaphore_wait(barrier, len(PARTNERS) + len(FAR_PARTNERS))

    def rows_of(j):
        return slice(j * tile, (j + 1) * tile)

    def a_copy(m, j):
        return rcopy(a_all.at[m, 0:tile], a_all.at[m, rows_of(j)], a_ss.at[m, j], a_rs.at[m, j], near(SHARE[m][j]))

    for m in range(2):
        for j in peers:
            a_copy(m, j).start()
    for c in range(n_chunk):
        b_load(1, c).start()
    for cp in so_load + bo_load + w_load:
        cp.start()
    for m in range(2):
        b_far_load(m).start()

    def g_copy(m, j, lo, size):
        return rcopy(gs.at[m, rows_of(j), lo:lo + size], g_out[m].at[:, pl.ds(pl.multiple_of(base + lo, CHUNK), size)],
                     g_ss.at[m, j], g_rs.at[m, j], near(SHARE[m][j]))

    def send_g(*portions):
        for m, c in portions:
            for j in links:
                g_copy(m, j, c * CHUNK, CHUNK).start()

    def rs_copy(m, j):
        return rcopy(rs_own.at[m, rows_of(j)], rs_in.at[m, rows_of(j)], rs_ss.at[m, j], rs_rs.at[m, j], near(SHARE[m][j]))

    def rf_copy(m, j):
        return rcopy(rs_own.at[m, rows_of(j)], rs_far.at[m, rows_of(j)], rf_ss.at[m, j], rf_rs.at[m, j], far(SHARE[m][j]))

    def ar_copy(m, j):
        return rcopy(ar_buf.at[m, rank], ar_buf.at[m, rank], ar_ss.at[m, j], ar_rs.at[m, j], near(CODE[j]))

    def rp_copy(m, j):
        return rcopy(rp_all.at[m, 0:tile], rp_all.at[m, rows_of(j)], rp_ss.at[m, j], rp_rs.at[m, j], near(SHARE[m][j]))

    def c_copy(m, j):
        return rcopy(cnew.at[m], c_out[m].at[:, pl.ds(base, block)], c_ss.at[m, j], c_rs.at[m, j], near(SHARE[m][j]))

    def sc_copy(j):
        return rcopy(sc_buf.at[0], sc_buf.at[j], sc_ss.at[j], sc_rs.at[j], near(CODE[j]))

    def sh_copy(j):
        return rcopy(sh_buf.at[0], sh_buf.at[j], sh_ss.at[j], sh_rs.at[j], near(SHARE[0][j]))

    def sf_copy(j):
        return rcopy(sh_buf.at[0], sf_buf.at[j], sf_ss.at[j], sf_rs.at[j], far(SHARE[0][j]))

    def products(m):
        for h in range(n_chunk // 2):
            for c in (2 * h, 2 * h + 1):
                b_load(m, c).wait()
            lanes = slice(2 * h * CHUNK, 2 * (h + 1) * CHUNK)
            g = jnp.dot(a_all[m], b_buf[m, :, lanes], preferred_element_type=F32)
            gs[m, :, lanes] = g
            sq = g * g
            ar_buf[m, rank, :, lanes] = jnp.sum(sq, axis=0, keepdims=True)
            part = fold(sq)
            rs_own[m] = part if h == 0 else rs_own[m] + part

    def products_far(m):
        b_far_load(m).wait()
        g_out[m][:, pl.ds(base_far, block)] = jnp.dot(a_all[m, 0:tile], b_far[m], preferred_element_type=F32)

    def send_sums(m):
        for j in peers:
            rs_copy(m, j).start()
        for j in range(N_BLOCK):
            rf_copy(m, j).start()
        for j in peers:
            ar_copy(m, j).start()

    with jax.named_scope('p01_a_wait0'):
        for j in peers:
            a_copy(0, j).wait_recv()
    with jax.named_scope('p02_products0'):
        products(0)
    send_sums(0)
    with jax.named_scope('p03_a_wait1'):
        for j in peers:
            a_copy(1, j).wait_recv()
    with jax.named_scope('p04_products1'):
        products(1)
    send_sums(1)
    send_g((0, 0))
    for m in range(2):
        g_out[m][:, pl.ds(base, block)] = gs[m, 0:tile]

    with jax.named_scope('p04_wsum'):
        for m in range(2):
            w_load[m].wait()

            def w_step(i, acc):
                blk = wv[m][:, pl.ds(pl.multiple_of(i * 1024, 1024), 1024)]
                return acc + fold(blk * blk)

            w_acc = lax.fori_loop(0, width // 1024, w_step, jnp.zeros((tile, 128), F32))
            sc_buf[0, 4 * m + 2:4 * m + 3, :] = jnp.sum(w_acc, axis=0, keepdims=True)
            bo_load[m].wait()
            so_load[m].wait()
        old0 = jnp.sum(so_buf[0], axis=1, keepdims=True) * (0.5 / 128)
        old1 = jnp.sum(bo_buf[1], axis=1, keepdims=True) * (1.0 / (64 * 128))
        sc_buf[0, 3:4, :] = jnp.broadcast_to(old0, (1, 128))
        sc_buf[0, 7:8, :] = jnp.broadcast_to(old1, (1, 128))
        for m in range(2):
            sc_buf[0, 4 * m + 1:4 * m + 2, :] = jnp.sum(rs_own[m], axis=0, keepdims=True)

    beta_two = hyper[0]
    rho_step = hyper[1]
    clip_max = hyper[2]
    eye = lax.broadcasted_iota(jnp.int32, (tile, tile), 0) == lax.broadcasted_iota(jnp.int32, (tile, tile), 1)
    for m in range(2):
        with jax.named_scope('p05_rs_wait%d' % m):
            for j in peers:
                rs_copy(m, j).wait_recv()
            for j in range(N_BLOCK):
                rf_copy(m, j).wait_recv()
        total = rs_own[m, 0:tile]
        for j in peers:
            total = total + rs_in[m, rows_of(j)]
        total_far = rs_far[m, 0:tile]
        for j in peers:
            total_far = total_far + rs_far[m, rows_of(j)]
        total = jnp.sum(total + total_far, axis=1, keepdims=True)
        old = jnp.sum(jnp.where(eye, jnp.broadcast_to(so_buf[m], (tile, tile)), 0.0), axis=1, keepdims=True)
        new = beta_two * old + (1.0 - beta_two) * (total * (1.0 / n_big) + EPS_ONE)
        rp_all[m, 0:tile] = jnp.broadcast_to(new, (tile, 128))
        r_out[m] = jnp.broadcast_to(new, (tile, 128))
        for j in peers:
            rp_copy(m, j).start()
    send_g((0, 1), (0, 2))

    with jax.named_scope('p06_far0'):
        products_far(0)
    for m in range(2):
        if m == 1:
            with jax.named_scope('p06_far1'):
                products_far(1)
        with jax.named_scope('p07_ar_wait%d' % m):
            for j in peers:
                ar_copy(m, j).wait()
        with jax.named_scope('p08_cnew%d' % m):
            total = ar_buf[m, 0]
            for j in peers:
                total = total + ar_buf[m, j]
            old = bo_buf[m, :, pl.ds(base, block)]
            new = beta_two * old + (1.0 - beta_two) * (total * (1.0 / n_small) + EPS_ONE)
            cnew[m] = new
            c_out[m][:, pl.ds(base, block)] = new
        for j in peers:
            c_copy(m, j).start()
        with jax.named_scope('p09_u%d' % m):
            def u_step(i, acc):
                lanes = pl.ds(pl.multiple_of(i * 512, 512), 512)
                blk = gs[m, :, lanes]
                return acc + fold(blk * blk * (1.0 / cnew[m, :, lanes]))

            u_acc = lax.fori_loop(0, block // 512, u_step, jnp.zeros((N_BLOCK * tile, 128), F32))
        with jax.named_scope('p10_rp%d' % m):
            for j in peers:
                rp_copy(m, j).wait()
        sc_buf[0, 4 * m:4 * m + 1, :] = jnp.sum(u_acc * SCALE / rp_all[m], axis=0, keepdims=True)

    for j in peers:
        sc_copy(j).start()
    send_g((0, 3), (1, 0), (1, 1))
    with jax.named_scope('p11_sc_wait'):
        for j in peers:
            sc_copy(j).wait()
    total = sc_buf[0]
    for j in peers:
        total = total + sc_buf[j]
    sh_buf[0] = total
    for j in peers:
        sh_copy(j).start()
    for j in range(N_BLOCK):
        sf_copy(j).start()
    send_g((1, 2), (1, 3))
    with jax.named_scope('p12_sh_wait'):
        for j in peers:
            sh_copy(j).wait()
        for j in range(N_BLOCK):
            sf_copy(j).wait()
    total = sh_buf[0] + sf_buf[0]
    for j in peers:
        total = total + (sh_buf[j] + sf_buf[j])
    sums = jnp.broadcast_to(jnp.sum(total, axis=1, keepdims=True), (8, 128))
    n_total = float(n_small) * float(n_big)
    for m, n_rows in ((0, n_small), (1, n_big)):
        u_sum, g_sum, w_sum, r_sum = (sums[4 * m + i:4 * m + i + 1] for i in range(4))
        row_mean = beta_two * (r_sum * (1.0 / n_rows)) + (1.0 - beta_two) * (g_sum * (1.0 / n_total) + EPS_ONE)
        upd_rms = jnp.sqrt(u_sum * row_mean * (1.0 / (n_total * SCALE)))
        w_rms = jnp.sqrt(w_sum * (1.0 / n_total))
        step_size = rho_step * jnp.maximum(EPS_TWO, w_rms) / jnp.maximum(1.0, upd_rms / clip_max)
        s_out[m:m + 1, :] = step_size * jnp.sqrt(row_mean)

    with jax.named_scope('p13_final'):
        for m in range(2):
            rf_copy(m, 0).wait_send()
            for j in peers:
                a_copy(m, j).wait_send()
                rs_copy(m, j).wait_send()
                rf_copy(m, j).wait_send()
                c_copy(m, j).wait()
            for j in links:
                g_copy(m, j, 0, block).wait()


def apply_kernel(g0, g1, w0, w1, c0, c1, r_new, scal, w0_new, w1_new, c0_new, c1_new, r0_new, r1_new,
                 w_buf, r_buf, w_sem, c_sem, r_sem):
    tile, width = w0.shape
    step = 4096
    eye = lax.broadcasted_iota(jnp.int32, (tile, tile), 0) == lax.broadcasted_iota(jnp.int32, (tile, tile), 1)
    c_new, r_out, w_new = (c0_new, c1_new), (r0_new, r1_new), (w0_new, w1_new)
    c_old = (c0, c1)
    copies = [pltpu.make_async_copy(c_old[m], c_new[m], c_sem.at[m]) for m in range(2)]
    for m in range(2):
        copies[m].start()
        r_buf[m] = jnp.sum(jnp.where(eye, r_new[m, :, 0:tile], 0.0), axis=0, keepdims=True)
    for m, (g, w, c) in enumerate(((g0, w0, c0), (g1, w1, c1))):
        row_scale = scal[m:m + 1, 0:1] * lax.rsqrt(r_new[m, :, 0:1])
        for i in range(width // step):
            lanes = slice(i * step, (i + 1) * step)
            w_buf[m, :, lanes] = w[:, lanes] - (g[:, lanes] * lax.rsqrt(c[:, lanes])) * row_scale
            copies.append(pltpu.make_async_copy(w_buf.at[m, :, lanes], w_new[m].at[:, lanes], w_sem.at[m, i]))
            copies[-1].start()
    for m in range(2):
        copies.append(pltpu.make_async_copy(r_buf.at[m], r_out[m], r_sem.at[m]))
        copies[-1].start()
    for cp in copies:
        cp.wait()


def solution(mesh):
    tile_in = P(None, 'row', 'col')
    tile_out = P(None, 'col', 'row')
    lane_row = P(None, None, 'row')
    lane_col = P(None, None, 'col')
    vec_row = P(None, 'row')
    vec_col = P(None, 'col')
    n_row = mesh.shape['row']
    n_col = mesh.shape['col']

    def local_step(hyper_params, w_in, x_in, dy_in, row_in, col_in, w_out, x_out, dy_out, row_out, col_out):
        tile, width = w_in.shape[1], w_in.shape[2]
        tokens = x_in.shape[1]
        block = width // N_BLOCK
        n_chunk = block // CHUNK
        dims = (tile, width, block, tile * n_row, width * n_col)
        rows = N_BLOCK * tile
        w0 = w_in[0]
        w1 = jnp.transpose(w_out[0])
        a0 = jnp.transpose(x_in[0])
        a1 = jnp.transpose(dy_out[0])
        dma = pltpu.SemaphoreType.DMA
        any_spec = pl.BlockSpec(memory_space=pl.ANY)
        hbm_spec = pl.BlockSpec(memory_space=pltpu.HBM)
        vmem_spec = pl.BlockSpec(memory_space=pltpu.VMEM)
        big = jax.ShapeDtypeStruct((tile, width), F32)
        vec = jax.ShapeDtypeStruct((1, width), F32)
        short = jax.ShapeDtypeStruct((1, tile), F32)
        g0, g1, c0, c1, wv0, wv1, r_new, scal = pl.pallas_call(
            functools.partial(stats_kernel, dims),
            out_shape=(big, big, vec, vec, big, big, jax.ShapeDtypeStruct((2, tile, 128), F32), jax.ShapeDtypeStruct((8, 128), F32)),
            in_specs=[pl.BlockSpec(memory_space=pltpu.SMEM)] + [hbm_spec] * 10,
            out_specs=(vmem_spec,) * 8,
            scratch_shapes=[
                pltpu.VMEM((2, rows, tokens), jnp.bfloat16),
                pltpu.VMEM((2, tokens, block), jnp.bfloat16),
                pltpu.VMEM((2, tokens, block), jnp.bfloat16),
                pltpu.VMEM((2, rows, block), F32),
                pltpu.VMEM((2, 1, tile), F32),
                pltpu.VMEM((2, 1, width), F32),
                pltpu.VMEM((2, N_BLOCK, 1, block), F32),
                pltpu.VMEM((2, 1, block), F32),
                pltpu.VMEM((2, rows, 128), F32),
                pltpu.VMEM((2, rows, 128), F32),
                pltpu.VMEM((2, rows, 128), F32),
                pltpu.VMEM((2, rows, 128), F32),
                pltpu.VMEM((N_BLOCK, 8, 128), F32),
                pltpu.VMEM((N_BLOCK, 8, 128), F32),
                pltpu.VMEM((N_BLOCK, 8, 128), F32),
                dma((2, n_chunk + 1)), dma((2,)), dma((8,)), dma((2,)),
            ] + [dma((2, 8))] * 14 + [dma((8,))] * 6,
            compiler_params=pltpu.CompilerParams(collective_id=0, has_side_effects=True, vmem_limit_bytes=40 * 1024 * 1024),
            name='stats',
        )(*[pltpu.with_memory_space_constraint(v, pltpu.HBM) for v in (hyper_params, a0, a1, row_in, col_out, col_in, row_out, dy_in[0], x_out[0], w0, w1)])

        n_step = width // 4096
        w0_new, w1_new, c0_new, c1_new, r0_new, r1_new = pl.pallas_call(
            apply_kernel,
            out_shape=(big, big, vec, vec, short, short),
            in_specs=[vmem_spec] * 8,
            out_specs=(hbm_spec,) * 6,
            scratch_shapes=[pltpu.VMEM((2, tile, width), F32), pltpu.VMEM((2, 1, tile), F32), dma((2, n_step)), dma((2,)), dma((2,))],
            compiler_params=pltpu.CompilerParams(vmem_limit_bytes=6 * 1024 * 1024),
            name='apply',
        )(g0, g1, wv0, wv1, c0, c1, r_new, scal)
        return w0_new[None], r0_new, c0_new, jnp.transpose(w1_new)[None], c1_new, r1_new

    return jax.shard_map(local_step, mesh=mesh, in_specs=(P(), tile_in, lane_row, lane_col, vec_row, vec_col, tile_out, lane_col, lane_row, vec_col, vec_row), out_specs=(tile_in, vec_row, vec_col, tile_out, vec_col, vec_row), check_vma=False)
```

time: 275 us -> 43.2 us (0.16)
  blocking collectives: 136 us -> 0 us
  matrix products: 49.6 us -> 0 us
  Pallas kernels: 0 us -> 42.4 us
  waiting for transfers between devices: 37.9 us -> 0 us
  between operations: 25.3 us -> 0.64 us
  other arithmetic: 22.6 us -> 0 us
    psum x3 -> x0, blocking collectives: 136 us -> none  [the longest x1 69 us: update_block(): scalar_sum = lax.psum(scalars, BOTH_AXES)]
    dot_general x2 -> x0, matrix products: 49.6 us -> none  [update_block(): lax.dot_general(x_blk, dy_blk, (((0,), (0,)), ((), ())), preferred_elemen...]
    pallas_call x0 -> x2, Pallas kernels: none -> 42.4 us  [the longest x1 40.1 us: local_step(): pl.pallas_call(functools.partial(stats_kernel, dims), out_shape=(big, big...]
    psum x1 -> x0, waiting for transfers between devices: 37.8 us -> none  [update_block(): col_sum = lax.psum(col_part, rows_axis)]
    another operation x4 -> x0, other arithmetic: 10 us -> none  [the longest x2 7.28 us: local_step(): jnp.stack([res_item[out_idx] for res_item in results])]
    reduce_sum x5 -> x0, other arithmetic: 7.43 us -> none  [the longest x2 4.18 us: update_block(): jnp.sum(w_blk * w_blk)]
    div x2 -> x0, other arithmetic: 2.95 us -> none  [update_block(): row_new / row_mean]
  transfers between devices with their start and end apart: 1 -> 0, of which waited for: 1 -> 0; matrix products, arithmetic and copies ran while one was open for 5% -> 0% of each run, Pallas kernels for 0% -> 0%
where the time goes in v2:
time: 43.2 us; the launch traced here: 43 us
  Pallas kernels  42.4 us (98%)
  between operations  0.64 us (1%)
    pallas_call x1, Pallas kernels, local_step(): pl.pallas_call(functools.partial(stats_kernel, dims), out_shape=(big, big...  40.1 us
    pallas_call x1, Pallas kernels, local_step(): pl.pallas_call(apply_kernel, out_shape=(big, big, vec, vec, short, short)...  2.33 us

profile of v2, /device:TPU:1, one launch (start us, length us, event | category | flops | bytes accessed | tf_op | source)
XLA Modules:
  0.0 43.0 jit_solution(5679425345935365665)
XLA Ops:
  0.6 40.1 %stats.1 = (f32[16,32768]{1,0:T(8,128)S(1)}, f32[16,32768]{1,0:T(8,128)S(1)}, f32[1,32768]{1,0:T(1,128)S(1)}, f32[1,32768]{1,0:T(1,128)S(1)}, f32[16,32768]{1,0:...) custom-call(f32[3]{0:T(128)} %hyper.1, bf16[16,1024]{1,0:T(8,128)(2,1)} %bitcast.18, ...), custom_call_target="tpu_custom_call" | custom-call | tf_op jit(solution)/shard_map/stats/pallas_call | solution.py:366
  40.7 2.3 %apply.1 = (f32[16,32768]{1,0:T(8,128)}, f32[16,32768]{1,0:T(8,128)}, f32[1,32768]{1,0:T(1,128)}, f32[1,32768]{1,0:T(1,128)}, f32[1,16]{1,0:T(1,128)}, /*index=5*/f32[1,16]{1,0:T(1,128)}) custom-call(f32[16,32768]{1,0:T(8,128)S(1)} %get-tuple-element.20.g0, f32[16,32768]{1,0:T(8,128)S(1)} %get-tuple-element.21.g1, f32[16,32768]{1,0:T(8,128)S(1)} %get-tuple-element.22.w0, ...), custom_call_target="tpu_custom_call" | custom-call | tf_op jit(solution)/shard_map/apply/pallas_call | solution.py:394

commit v3 on v2

v3 whole, which is shorter than its diff:
```python
import functools

import jax
import jax.numpy as jnp
from jax import lax
from jax.experimental import pallas as pl
from jax.experimental.pallas import tpu as pltpu
from jax.sharding import PartitionSpec as P

EPS_ONE = 1e-30
EPS_TWO = 1e-3
MESH = pl.DeviceIdType.MESH
F32 = jnp.float32

SHARE = ((0, 1, 3, 4, 12, 16, 48, 5), (0, 1, 3, 4, 12, 16, 48, 60))
CODE = (0, 14, 33, 55, 24, 22, 57, 47)
PARTNERS = tuple(sorted({m for lst in SHARE for m in lst[1:]} | set(CODE[1:])))
FAR_PARTNERS = tuple(sorted({m for lst in SHARE for m in lst}))
N_BLOCK = 8
CHUNK = 1024
SCALE = 2.0 ** -20


def digit_xor(v, m):
    if m == 0:
        return v
    if m == 1:
        return v + 1 - 2 * (v % 2)
    if m == 2:
        return (v + 2) % 4
    return 3 - v


def fold(x):
    acc = x[:, 0:128]
    for i in range(1, x.shape[1] // 128):
        acc = acc + x[:, i * 128:(i + 1) * 128]
    return acc


def stats_kernel(dims, hyper_in, a0, a1, so0, so1, bo0, bo1, b0, b1, w0, w1,
                 g0, g1, c0, c1, wv0, wv1, r_out, s_out,
                 hyper, a_all, b_buf, b_far, gs, so_buf, bo_buf, ar_buf, cnew, rs_own, rs_in, rp_all,
                 sc_buf, sh_buf,
                 sem_b, sem_w, sem_in, sem_pair, sem_one):
    tile, width, block, n_small, n_big = dims
    n_chunk = block // CHUNK
    col = lax.axis_index('col')
    row = lax.axis_index('row')
    x, y, z = row % 4, (row // 4) % 4, row // 16
    bx, by, bz = x // 2, y // 2, z // 2
    ax, ay, az = (x + bx) % 2, (y + by) % 2, (z + bz) % 2
    syn = (ax + by + az) % 2 + 2 * ((bx + ay + by) % 2) + 4 * ((ay + az + bz) % 2)
    rank = bx + 2 * bz + 4 * ay
    base = pl.multiple_of(syn * block, block)
    base_far = pl.multiple_of((N_BLOCK - 1 - syn) * block, block)
    peers = (N_BLOCK - 1,) + tuple(range(1, N_BLOCK - 1))
    a_rs, g_rs, rs_rs, rp_rs, c_rs, ar_rs = (lambda m, i=i: sem_pair.at[i, m] for i in range(6))
    a_ss, g_ss, rs_ss, rp_ss, c_ss, ar_ss, sc_ss, sh_ss, sc_rs, sh_rs = (sem_one.at[i] for i in range(10))
    links = range(1, N_BLOCK - 1)

    def peer_row(mask):
        return digit_xor(z, mask // 16) * 16 + digit_xor(y, (mask // 4) % 4) * 4 + digit_xor(x, mask % 4)

    def near(mask):
        return (col, peer_row(mask))

    def far(mask):
        return (1 - col, peer_row(mask))

    a_in, so_in, bo_in, b_in, w_in = (a0, a1), (so0, so1), (bo0, bo1), (b0, b1), (w0, w1)
    g_out, c_out, wv = (g0, g1), (c0, c1), (wv0, wv1)

    def rcopy(src, dst, ss, rs, dev):
        return pltpu.make_async_remote_copy(src_ref=src, dst_ref=dst, send_sem=ss, recv_sem=rs, device_id=dev, device_id_type=MESH)

    barrier = pltpu.get_barrier_semaphore()
    for mask in PARTNERS:
        pl.semaphore_signal(barrier, inc=1, device_id=near(mask), device_id_type=MESH)
    for mask in FAR_PARTNERS:
        pl.semaphore_signal(barrier, inc=1, device_id=far(mask), device_id_type=MESH)

    def drain(ref, sem):
        pltpu.make_async_copy(ref, ref, sem).wait()

    a_load = [pltpu.make_async_copy(a_in[m], a_all.at[m, 0:tile], sem_in.at[0]) for m in range(2)]
    for cp in a_load:
        cp.start()

    def b_load(m, c):
        return pltpu.make_async_copy(b_in[m].at[:, pl.ds(pl.multiple_of(base + c * CHUNK, CHUNK), CHUNK)],
                                     b_buf.at[m, :, c * CHUNK:(c + 1) * CHUNK], sem_b.at[m])

    def b_far_load(m):
        return pltpu.make_async_copy(b_in[m].at[:, pl.ds(base_far, block)], b_far.at[m], sem_b.at[2 + m])

    so_load = [pltpu.make_async_copy(so_in[m], so_buf.at[m], sem_in.at[1]) for m in range(2)]
    bo_load = [pltpu.make_async_copy(bo_in[m], bo_buf.at[m], sem_in.at[2]) for m in range(2)]
    w_load = [pltpu.make_async_copy(w_in[m], wv[m], sem_w.at[m]) for m in range(2)]
    hyper_load = pltpu.make_async_copy(hyper_in, hyper, sem_in.at[3])
    hyper_load.start()
    drain(a_all.at[:, 0:tile], sem_in.at[0])
    for c in range(n_chunk):
        b_load(0, c).start()
    with jax.named_scope('p00_barrier'):
        pl.semaphore_wait(barrier, len(PARTNERS) + len(FAR_PARTNERS))

    def rows_of(j):
        return slice(j * tile, (j + 1) * tile)

    def a_copy(m, j):
        return rcopy(a_all.at[m, 0:tile], a_all.at[m, rows_of(j)], a_ss, a_rs(m), near(SHARE[m][j]))

    for m in range(2):
        for j in peers:
            a_copy(m, j).start()
    for c in range(n_chunk):
        b_load(1, c).start()
    for cp in so_load + bo_load + w_load:
        cp.start()

    def g_copy(m, j, lo, size):
        return rcopy(gs.at[m, rows_of(j), lo:lo + size], g_out[m].at[:, pl.ds(pl.multiple_of(base + lo, CHUNK), size)],
                     g_ss, g_rs(m), near(SHARE[m][j]))

    def send_g(*portions):
        for m, c in portions:
            for j in links:
                g_copy(m, j, c * CHUNK, CHUNK).start()

    def rs_copy(m, j):
        return rcopy(rs_own.at[m, rows_of(j)], rs_in.at[m, rows_of(j)], rs_ss, rs_rs(m), near(SHARE[m][j]))

    def rf_copy(m, j):
        return rcopy(rs_own.at[m, rows_of(j)], rs_in.at[m, rows_of(N_BLOCK + j)], rs_ss, rs_rs(m), far(SHARE[m][j]))

    def ar_copy(m, j):
        return rcopy(ar_buf.at[m, rank], ar_buf.at[m, rank], ar_ss, ar_rs(m), near(CODE[j]))

    def rp_copy(m, j):
        return rcopy(rp_all.at[m, 0:tile], rp_all.at[m, rows_of(j)], rp_ss, rp_rs(m), near(SHARE[m][j]))

    def c_copy(m, j):
        return rcopy(cnew.at[m], c_out[m].at[:, pl.ds(base, block)], c_ss, c_rs(m), near(SHARE[m][j]))

    def sc_copy(j):
        return rcopy(sc_buf.at[0], sc_buf.at[j], sc_ss, sc_rs, near(CODE[j]))

    def sh_copy(j):
        return rcopy(sh_buf.at[0], sh_buf.at[j], sh_ss, sh_rs, near(SHARE[0][j]))

    def sf_copy(j):
        return rcopy(sh_buf.at[0], sh_buf.at[N_BLOCK + j], sh_ss, sh_rs, far(SHARE[0][j]))

    def products(m):
        drain(b_buf.at[m], sem_b.at[m])
        for h in range(n_chunk // 2):
            lanes = slice(2 * h * CHUNK, 2 * (h + 1) * CHUNK)
            g = jnp.dot(a_all[m], b_buf[m, :, lanes], preferred_element_type=F32)
            gs[m, :, lanes] = g
            sq = g * g
            ar_buf[m, rank, :, lanes] = jnp.sum(sq, axis=0, keepdims=True)
            part = fold(sq)
            rs_own[m] = part if h == 0 else rs_own[m] + part

    def products_far(m):
        b_far_load(m).wait()
        g_out[m][:, pl.ds(base_far, block)] = jnp.dot(a_all[m, 0:tile], b_far[m], preferred_element_type=F32)

    def send_sums(m):
        for j in peers:
            rs_copy(m, j).start()
        for j in peers + (0,):
            rf_copy(m, j).start()
        for j in peers:
            ar_copy(m, j).start()

    with jax.named_scope('p01_a_wait0'):
        drain(a_all.at[0, tile:N_BLOCK * tile], a_rs(0))
    with jax.named_scope('p02_products0'):
        products(0)
    send_sums(0)
    with jax.named_scope('p03_a_wait1'):
        drain(a_all.at[1, tile:N_BLOCK * tile], a_rs(1))
    with jax.named_scope('p04_products1'):
        products(1)
    send_sums(1)
    for m in range(2):
        b_far_load(m).start()
    for m in range(2):
        g_out[m][:, pl.ds(base, block)] = gs[m, 0:tile]

    with jax.named_scope('p04_wsum'):
        for m in range(2):
            w_load[m].wait()

            def w_step(i, acc):
                blk = wv[m][:, pl.ds(pl.multiple_of(i * 1024, 1024), 1024)]
                return acc + fold(blk * blk)

            w_acc = lax.fori_loop(0, width // 1024, w_step, jnp.zeros((tile, 128), F32))
            sc_buf[0, 4 * m + 2:4 * m + 3, :] = jnp.sum(w_acc, axis=0, keepdims=True)
        drain(so_buf, sem_in.at[1])
        drain(bo_buf, sem_in.at[2])
        old0 = jnp.sum(so_buf[0], axis=1, keepdims=True) * (0.5 / 128)
        old1 = jnp.sum(bo_buf[1], axis=1, keepdims=True) * (1.0 / (64 * 128))
        sc_buf[0, 3:4, :] = jnp.broadcast_to(old0, (1, 128))
        sc_buf[0, 7:8, :] = jnp.broadcast_to(old1, (1, 128))
        for m in range(2):
            sc_buf[0, 4 * m + 1:4 * m + 2, :] = jnp.sum(rs_own[m], axis=0, keepdims=True)

    hyper_load.wait()
    beta_two = hyper[0]
    rho_step = hyper[1]
    clip_max = hyper[2]
    eye = lax.broadcasted_iota(jnp.int32, (tile, tile), 0) == lax.broadcasted_iota(jnp.int32, (tile, tile), 1)
    for m in range(2):
        with jax.named_scope('p05_rs_wait%d' % m):
            drain(rs_in.at[m, tile:2 * N_BLOCK * tile], rs_rs(m))
        total = rs_own[m, 0:tile]
        for j in range(1, N_BLOCK):
            total = total + rs_in[m, rows_of(j)]
        total_far = rs_in[m, rows_of(N_BLOCK)]
        for j in range(1, N_BLOCK):
            total_far = total_far + rs_in[m, rows_of(N_BLOCK + j)]
        total = jnp.sum(total + total_far, axis=1, keepdims=True)
        old = jnp.sum(jnp.where(eye, jnp.broadcast_to(so_buf[m], (tile, tile)), 0.0), axis=1, keepdims=True)
        new = beta_two * old + (1.0 - beta_two) * (total * (1.0 / n_big) + EPS_ONE)
        rp_all[m, 0:tile] = jnp.broadcast_to(new, (tile, 128))
        r_out[m] = jnp.broadcast_to(new, (tile, 128))
        for j in peers:
            rp_copy(m, j).start()
    send_g((0, 0), (0, 1))

    for m in range(2):
        with jax.named_scope('p07_ar_wait%d' % m):
            drain(ar_buf.at[m, 1:N_BLOCK], ar_rs(m))
        with jax.named_scope('p08_cnew%d' % m):
            total = ar_buf[m, 0]
            for j in range(1, N_BLOCK):
                total = total + ar_buf[m, j]
            old = bo_buf[m, :, pl.ds(base, block)]
            new = beta_two * old + (1.0 - beta_two) * (total * (1.0 / n_small) + EPS_ONE)
            cnew[m] = new
            c_out[m][:, pl.ds(base, block)] = new
        for j in peers:
            c_copy(m, j).start()
        with jax.named_scope('p09_u%d' % m):
            def u_step(i, acc):
                lanes = pl.ds(pl.multiple_of(i * 512, 512), 512)
                blk = gs[m, :, lanes]
                return acc + fold(blk * blk * (1.0 / cnew[m, :, lanes]))

            u_acc = lax.fori_loop(0, block // 512, u_step, jnp.zeros((N_BLOCK * tile, 128), F32))
        with jax.named_scope('p10_rp%d' % m):
            drain(rp_all.at[m, tile:N_BLOCK * tile], rp_rs(m))
        sc_buf[0, 4 * m:4 * m + 1, :] = jnp.sum(u_acc * SCALE / rp_all[m], axis=0, keepdims=True)

    for j in peers:
        sc_copy(j).start()
    send_g((0, 2), (0, 3), (1, 0), (1, 1))
    with jax.named_scope('p11_far'):
        products_far(0)
        products_far(1)
    with jax.named_scope('p11_sc_wait'):
        drain(sc_buf.at[1:N_BLOCK], sc_rs)
        drain(sc_buf.at[1:N_BLOCK], sc_ss)
    total = sc_buf[0]
    for j in peers:
        total = total + sc_buf[j]
    sh_buf[0] = total
    for j in peers:
        sh_copy(j).start()
    for j in peers + (0,):
        sf_copy(j).start()
    send_g((1, 2), (1, 3))
    with jax.named_scope('p12_sh_wait'):
        drain(sh_buf.at[1:2 * N_BLOCK], sh_rs)
    total = sh_buf[0]
    for j in range(1, 2 * N_BLOCK):
        total = total + sh_buf[j]
    sums = jnp.broadcast_to(jnp.sum(total, axis=1, keepdims=True), (8, 128))
    n_total = float(n_small) * float(n_big)
    for m, n_rows in ((0, n_small), (1, n_big)):
        u_sum, g_sum, w_sum, r_sum = (sums[4 * m + i:4 * m + i + 1] for i in range(4))
        row_mean = beta_two * (r_sum * (1.0 / n_rows)) + (1.0 - beta_two) * (g_sum * (1.0 / n_total) + EPS_ONE)
        upd_rms = jnp.sqrt(u_sum * row_mean * (1.0 / (n_total * SCALE)))
        w_rms = jnp.sqrt(w_sum * (1.0 / n_total))
        step_size = rho_step * jnp.maximum(EPS_TWO, w_rms) / jnp.maximum(1.0, upd_rms / clip_max)
        s_out[m:m + 1, :] = step_size * jnp.sqrt(row_mean)

    with jax.named_scope('p13_final'):
        n_link = len(links)
        for m in range(2):
            drain(c_out[m].at[:, 0:(N_BLOCK - 1) * block], c_rs(m))
            drain(g_out[m].at[:, 0:n_link * block], g_rs(m))
        drain(a_all.at[:, tile:N_BLOCK * tile], a_ss)
        drain(rs_in.at[:, tile:2 * N_BLOCK * tile], rs_ss)
        drain(rp_all.at[:, tile:N_BLOCK * tile], rp_ss)
        drain(ar_buf.at[:, 1:N_BLOCK], ar_ss)
        for m in range(2):
            drain(c_out[m].at[:, 0:(N_BLOCK - 1) * block], c_ss)
        drain(gs.at[:, tile:(1 + n_link) * tile], g_ss)
        drain(sh_buf.at[1:2 * N_BLOCK], sh_ss)


def apply_kernel(g0, g1, w0, w1, c0, c1, r_new, scal, w0_new, w1_new, c0_new, c1_new, r0_new, r1_new,
                 w_buf, r_buf, sems):
    tile, width = w0.shape
    step = 4096
    eye = lax.broadcasted_iota(jnp.int32, (tile, tile), 0) == lax.broadcasted_iota(jnp.int32, (tile, tile), 1)
    c_new, r_out, w_new = (c0_new, c1_new), (r0_new, r1_new), (w0_new, w1_new)
    c_old = (c0, c1)
    for m in range(2):
        pltpu.make_async_copy(c_old[m], c_new[m], sems.at[2]).start()
        r_buf[m] = jnp.sum(jnp.where(eye, r_new[m, :, 0:tile], 0.0), axis=0, keepdims=True)
    for m, (g, w, c) in enumerate(((g0, w0, c0), (g1, w1, c1))):
        row_scale = scal[m:m + 1, 0:1] * lax.rsqrt(r_new[m, :, 0:1])
        for i in range(width // step):
            lanes = slice(i * step, (i + 1) * step)
            w_buf[m, :, lanes] = w[:, lanes] - (g[:, lanes] * lax.rsqrt(c[:, lanes])) * row_scale
            pltpu.make_async_copy(w_buf.at[m, :, lanes], w_new[m].at[:, lanes], sems.at[m]).start()
    for m in range(2):
        pltpu.make_async_copy(r_buf.at[m], r_out[m], sems.at[3]).start()
    for m in range(2):
        pltpu.make_async_copy(w_buf.at[m], w_new[m], sems.at[m]).wait()
    for m in range(2):
        pltpu.make_async_copy(c_old[m], c_new[m], sems.at[2]).wait()
    for m in range(2):
        pltpu.make_async_copy(r_buf.at[m], r_out[m], sems.at[3]).wait()


def solution(mesh):
    tile_in = P(None, 'row', 'col')
    tile_out = P(None, 'col', 'row')
    lane_row = P(None, None, 'row')
    lane_col = P(None, None, 'col')
    vec_row = P(None, 'row')
    vec_col = P(None, 'col')
    n_row = mesh.shape['row']
    n_col = mesh.shape['col']

    def local_step(hyper_params, w_in, x_in, dy_in, row_in, col_in, w_out, x_out, dy_out, row_out, col_out):
        tile, width = w_in.shape[1], w_in.shape[2]
        tokens = x_in.shape[1]
        block = width // N_BLOCK
        n_chunk = block // CHUNK
        dims = (tile, width, block, tile * n_row, width * n_col)
        rows = N_BLOCK * tile
        w0 = w_in[0]
        w1 = jnp.transpose(w_out[0])
        a0 = jnp.transpose(x_in[0])
        a1 = jnp.transpose(dy_out[0])
        dma = pltpu.SemaphoreType.DMA
        any_spec = pl.BlockSpec(memory_space=pl.ANY)
        hbm_spec = pl.BlockSpec(memory_space=pltpu.HBM)
        vmem_spec = pl.BlockSpec(memory_space=pltpu.VMEM)
        big = jax.ShapeDtypeStruct((tile, width), F32)
        vec = jax.ShapeDtypeStruct((1, width), F32)
        short = jax.ShapeDtypeStruct((1, tile), F32)
        g0, g1, c0, c1, wv0, wv1, r_new, scal = pl.pallas_call(
            functools.partial(stats_kernel, dims),
            out_shape=(big, big, vec, vec, big, big, jax.ShapeDtypeStruct((2, tile, 128), F32), jax.ShapeDtypeStruct((8, 128), F32)),
            in_specs=[hbm_spec] * 11,
            out_specs=(vmem_spec,) * 8,
            scratch_shapes=[
                pltpu.SMEM((3,), F32),
                pltpu.VMEM((2, rows, tokens), jnp.bfloat16),
                pltpu.VMEM((2, tokens, block), jnp.bfloat16),
                pltpu.VMEM((2, tokens, block), jnp.bfloat16),
                pltpu.VMEM((2, rows, block), F32),
                pltpu.VMEM((2, 1, tile), F32),
                pltpu.VMEM((2, 1, width), F32),
                pltpu.VMEM((2, N_BLOCK, 1, block), F32),
                pltpu.VMEM((2, 1, block), F32),
                pltpu.VMEM((2, rows, 128), F32),
                pltpu.VMEM((2, 2 * rows, 128), F32),
                pltpu.VMEM((2, rows, 128), F32),
                pltpu.VMEM((N_BLOCK, 8, 128), F32),
                pltpu.VMEM((2 * N_BLOCK, 8, 128), F32),
                dma((4,)), dma((2,)), dma((4,)), dma((6, 2)), dma((10,)),
            ],
            compiler_params=pltpu.CompilerParams(collective_id=0, has_side_effects=True, vmem_limit_bytes=40 * 1024 * 1024),
            name='stats',
        )(*[pltpu.with_memory_space_constraint(v, pltpu.HBM) for v in (hyper_params, a0, a1, row_in, col_out, col_in, row_out, dy_in[0], x_out[0], w0, w1)])

        w0_new, w1_new, c0_new, c1_new, r0_new, r1_new = pl.pallas_call(
            apply_kernel,
            out_shape=(big, big, vec, vec, short, short),
            in_specs=[vmem_spec] * 8,
            out_specs=(hbm_spec,) * 6,
            scratch_shapes=[pltpu.VMEM((2, tile, width), F32), pltpu.VMEM((2, 1, tile), F32), dma((4,))],
            compiler_params=pltpu.CompilerParams(vmem_limit_bytes=6 * 1024 * 1024),
            name='apply',
        )(g0, g1, wv0, wv1, c0, c1, r_new, scal)
        return w0_new[None], r0_new, c0_new, jnp.transpose(w1_new)[None], c1_new, r1_new

    return jax.shard_map(local_step, mesh=mesh, in_specs=(P(), tile_in, lane_row, lane_col, vec_row, vec_col, tile_out, lane_col, lane_row, vec_col, vec_row), out_specs=(tile_in, vec_row, vec_col, tile_out, vec_col, vec_row), check_vma=False)
```

time: 43.2 us -> 40.5 us (0.937)
  Pallas kernels: 42.4 us -> 39.7 us
    pallas_call x1, Pallas kernels: 40.1 us -> 37.6 us  [local_step(): pl.pallas_call(functools.partial(stats_kernel, dims), out_shape=(big, big...]
where the time goes in v3:
time: 40.5 us; the launch traced here: 40.3 us
  Pallas kernels  39.7 us (98%)
  between operations  0.64 us (2%)
    pallas_call x1, Pallas kernels, local_step(): pl.pallas_call(functools.partial(stats_kernel, dims), out_shape=(big, big...  37.6 us
    pallas_call x1, Pallas kernels, local_step(): pl.pallas_call(apply_kernel, out_shape=(big, big, vec, vec, short, short)...  2.14 us

profile of v3, /device:TPU:1, one launch (start us, length us, event | category | flops | bytes accessed | tf_op | source)
XLA Modules:
  0.0 40.3 jit_solution(4323533769298209126)
XLA Ops:
  0.6 37.6 %stats.1 = (f32[16,32768]{1,0:T(8,128)S(1)}, f32[16,32768]{1,0:T(8,128)S(1)}, f32[1,32768]{1,0:T(1,128)S(1)}, f32[1,32768]{1,0:T(1,128)S(1)}, f32[16,32768]{1,0:...) custom-call(f32[3]{0:T(128)} %hyper_in.1, bf16[16,1024]{1,0:T(8,128)(2,1)} %bitcast.18, ...), custom_call_target="tpu_custom_call" | custom-call | tf_op jit(solution)/shard_map/stats/pallas_call | solution.py:361
  38.2 2.1 %apply.1 = (f32[16,32768]{1,0:T(8,128)}, f32[16,32768]{1,0:T(8,128)}, f32[1,32768]{1,0:T(1,128)}, f32[1,32768]{1,0:T(1,128)}, f32[1,16]{1,0:T(1,128)}, /*index=5*/f32[1,16]{1,0:T(1,128)}) custom-call(f32[16,32768]{1,0:T(8,128)S(1)} %get-tuple-element.20.g0, f32[16,32768]{1,0:T(8,128)S(1)} %get-tuple-element.21.g1, f32[16,32768]{1,0:T(8,128)S(1)} %get-tuple-element.22.w0, ...), custom_call_target="tpu_custom_call" | custom-call | tf_op jit(solution)/shard_map/apply/pallas_call | solution.py:387

commit v4 on v3

--- a/solution.py
+++ b/solution.py
@@ -14,7 +14,7 @@
 
 SHARE = ((0, 1, 3, 4, 12, 16, 48, 5), (0, 1, 3, 4, 12, 16, 48, 60))
 CODE = (0, 14, 33, 55, 24, 22, 57, 47)
-PARTNERS = tuple(sorted({m for lst in SHARE for m in lst[1:]} | set(CODE[1:])))
+PARTNERS = tuple(sorted({m for lst in SHARE for m in lst[1:]} | {2, 7, 8, 19, 32}))
 FAR_PARTNERS = tuple(sorted({m for lst in SHARE for m in lst}))
 N_BLOCK = 8
 CHUNK = 1024
@@ -172,6 +172,8 @@
             rs_copy(m, j).start()
         for j in peers + (0,):
             rf_copy(m, j).start()
+
+    def send_cols(m):
         for j in peers:
             ar_copy(m, j).start()
 
@@ -182,9 +184,13 @@
     send_sums(0)
     with jax.named_scope('p03_a_wait1'):
         drain(a_all.at[1, tile:N_BLOCK * tile], a_rs(1))
+    send_cols(0)
+    send_g((0, 0))
     with jax.named_scope('p04_products1'):
         products(1)
     send_sums(1)
+    send_cols(1)
+    send_g((0, 1))
     for m in range(2):
         b_far_load(m).start()
     for m in range(2):
@@ -230,7 +236,7 @@
         r_out[m] = jnp.broadcast_to(new, (tile, 128))
         for j in peers:
             rp_copy(m, j).start()
-    send_g((0, 0), (0, 1))
+    send_g((0, 2), (0, 3))
 
     for m in range(2):
         with jax.named_scope('p07_ar_wait%d' % m):
@@ -258,7 +264,7 @@
 
     for j in peers:
         sc_copy(j).start()
-    send_g((0, 2), (0, 3), (1, 0), (1, 1))
+    send_g((1, 0), (1, 1), (1, 2))
     with jax.named_scope('p11_far'):
         products_far(0)
         products_far(1)
@@ -273,7 +279,7 @@
         sh_copy(j).start()
     for j in peers + (0,):
         sf_copy(j).start()
-    send_g((1, 2), (1, 3))
+    send_g((1, 3))
     with jax.named_scope('p12_sh_wait'):
         drain(sh_buf.at[1:2 * N_BLOCK], sh_rs)
     total = sh_buf[0]

time: 40.5 us -> 37.5 us (0.926)
  Pallas kernels: 39.7 us -> 36.7 us
    pallas_call x1, Pallas kernels: 37.6 us -> 34.5 us  [local_step(): pl.pallas_call(functools.partial(stats_kernel, dims), out_shape=(big, big...]
where the time goes in v4:
time: 37.5 us; the launch traced here: 37.3 us
  Pallas kernels  36.7 us (98%)
  between operations  0.64 us (2%)
    pallas_call x1, Pallas kernels, local_step(): pl.pallas_call(functools.partial(stats_kernel, dims), out_shape=(big, big...  34.5 us
    pallas_call x1, Pallas kernels, local_step(): pl.pallas_call(apply_kernel, out_shape=(big, big, vec, vec, short, short)...  2.14 us

profile of v4, /device:TPU:1, one launch (start us, length us, event | category | flops | bytes accessed | tf_op | source)
XLA Modules:
  0.0 37.3 jit_solution(15434666651737336460)
XLA Ops:
  0.6 34.5 %stats.1 = (f32[16,32768]{1,0:T(8,128)S(1)}, f32[16,32768]{1,0:T(8,128)S(1)}, f32[1,32768]{1,0:T(1,128)S(1)}, f32[1,32768]{1,0:T(1,128)S(1)}, f32[16,32768]{1,0:...) custom-call(f32[3]{0:T(128)} %hyper_in.1, bf16[16,1024]{1,0:T(8,128)(2,1)} %bitcast.18, ...), custom_call_target="tpu_custom_call" | custom-call | tf_op jit(solution)/shard_map/stats/pallas_call | solution.py:367
  35.2 2.1 %apply.1 = (f32[16,32768]{1,0:T(8,128)}, f32[16,32768]{1,0:T(8,128)}, f32[1,32768]{1,0:T(1,128)}, f32[1,32768]{1,0:T(1,128)}, f32[1,16]{1,0:T(1,128)}, /*index=5*/f32[1,16]{1,0:T(1,128)}) custom-call(f32[16,32768]{1,0:T(8,128)S(1)} %get-tuple-element.20.g0, f32[16,32768]{1,0:T(8,128)S(1)} %get-tuple-element.21.g1, f32[16,32768]{1,0:T(8,128)S(1)} %get-tuple-element.22.w0, ...), custom_call_target="tpu_custom_call" | custom-call | tf_op jit(solution)/shard_map/apply/pallas_call | solution.py:393

commit v5 on v4

--- a/solution.py
+++ b/solution.py
@@ -15,7 +15,6 @@
 SHARE = ((0, 1, 3, 4, 12, 16, 48, 5), (0, 1, 3, 4, 12, 16, 48, 60))
 CODE = (0, 14, 33, 55, 24, 22, 57, 47)
 PARTNERS = tuple(sorted({m for lst in SHARE for m in lst[1:]} | {2, 7, 8, 19, 32}))
-FAR_PARTNERS = tuple(sorted({m for lst in SHARE for m in lst}))
 N_BLOCK = 8
 CHUNK = 1024
 SCALE = 2.0 ** -20
@@ -77,8 +76,7 @@
     barrier = pltpu.get_barrier_semaphore()
     for mask in PARTNERS:
         pl.semaphore_signal(barrier, inc=1, device_id=near(mask), device_id_type=MESH)
-    for mask in FAR_PARTNERS:
-        pl.semaphore_signal(barrier, inc=1, device_id=far(mask), device_id_type=MESH)
+    pl.semaphore_signal(barrier, inc=1, device_id=far(0), device_id_type=MESH)
 
     def drain(ref, sem):
         pltpu.make_async_copy(ref, ref, sem).wait()
@@ -103,7 +101,7 @@
     for c in range(n_chunk):
         b_load(0, c).start()
     with jax.named_scope('p00_barrier'):
-        pl.semaphore_wait(barrier, len(PARTNERS) + len(FAR_PARTNERS))
+        pl.semaphore_wait(barrier, len(PARTNERS) + 1)
 
     def rows_of(j):
         return slice(j * tile, (j + 1) * tile)
@@ -168,10 +166,10 @@
         g_out[m][:, pl.ds(base_far, block)] = jnp.dot(a_all[m, 0:tile], b_far[m], preferred_element_type=F32)
 
     def send_sums(m):
+        for j in peers + (0,):
+            rf_copy(m, j).start()
         for j in peers:
             rs_copy(m, j).start()
-        for j in peers + (0,):
-            rf_copy(m, j).start()
 
     def send_cols(m):
         for j in peers:
@@ -185,12 +183,10 @@
     with jax.named_scope('p03_a_wait1'):
         drain(a_all.at[1, tile:N_BLOCK * tile], a_rs(1))
     send_cols(0)
-    send_g((0, 0))
     with jax.named_scope('p04_products1'):
         products(1)
     send_sums(1)
     send_cols(1)
-    send_g((0, 1))
     for m in range(2):
         b_far_load(m).start()
     for m in range(2):
@@ -236,7 +232,9 @@
         r_out[m] = jnp.broadcast_to(new, (tile, 128))
         for j in peers:
             rp_copy(m, j).start()
-    send_g((0, 2), (0, 3))
+        if m == 0:
+            send_g((0, 0))
+    send_g((0, 1), (0, 2))
 
     for m in range(2):
         with jax.named_scope('p07_ar_wait%d' % m):
@@ -264,7 +262,7 @@
 
     for j in peers:
         sc_copy(j).start()
-    send_g((1, 0), (1, 1), (1, 2))
+    send_g((0, 3), (1, 0), (1, 1))
     with jax.named_scope('p11_far'):
         products_far(0)
         products_far(1)
@@ -275,11 +273,11 @@
     for j in peers:
         total = total + sc_buf[j]
     sh_buf[0] = total
+    for j in peers + (0,):
+        sf_copy(j).start()
     for j in peers:
         sh_copy(j).start()
-    for j in peers + (0,):
-        sf_copy(j).start()
-    send_g((1, 3))
+    send_g((1, 2), (1, 3))
     with jax.named_scope('p12_sh_wait'):
         drain(sh_buf.at[1:2 * N_BLOCK], sh_rs)
     total = sh_buf[0]

time: 37.5 us -> 36.3 us (0.968)
  Pallas kernels: 36.7 us -> 35.1 us
    pallas_call x1, Pallas kernels: 34.5 us -> 33 us  [local_step(): pl.pallas_call(functools.partial(stats_kernel, dims), out_shape=(big, big...]
where the time goes in v5:
time: 36.3 us; the launch traced here: 35.8 us
  Pallas kernels  35.1 us (97%)
  between operations  0.64 us (2%)
    pallas_call x1, Pallas kernels, local_step(): pl.pallas_call(functools.partial(stats_kernel, dims), out_shape=(big, big...  33 us
    pallas_call x1, Pallas kernels, local_step(): pl.pallas_call(apply_kernel, out_shape=(big, big, vec, vec, short, short)...  2.14 us

profile of v5, /device:TPU:1, one launch (start us, length us, event | category | flops | bytes accessed | tf_op | source)
XLA Modules:
  0.0 35.8 jit_solution(14721480018958937127)
XLA Ops:
  0.6 33.0 %stats.1 = (f32[16,32768]{1,0:T(8,128)S(1)}, f32[16,32768]{1,0:T(8,128)S(1)}, f32[1,32768]{1,0:T(1,128)S(1)}, f32[1,32768]{1,0:T(1,128)S(1)}, f32[16,32768]{1,0:...) custom-call(f32[3]{0:T(128)} %hyper_in.1, bf16[16,1024]{1,0:T(8,128)(2,1)} %bitcast.18, ...), custom_call_target="tpu_custom_call" | custom-call | tf_op jit(solution)/shard_map/stats/pallas_call | solution.py:365
  33.6 2.1 %apply.1 = (f32[16,32768]{1,0:T(8,128)}, f32[16,32768]{1,0:T(8,128)}, f32[1,32768]{1,0:T(1,128)}, f32[1,32768]{1,0:T(1,128)}, f32[1,16]{1,0:T(1,128)}, /*index=5*/f32[1,16]{1,0:T(1,128)}) custom-call(f32[16,32768]{1,0:T(8,128)S(1)} %get-tuple-element.20.g0, f32[16,32768]{1,0:T(8,128)S(1)} %get-tuple-element.21.g1, f32[16,32768]{1,0:T(8,128)S(1)} %get-tuple-element.22.w0, ...), custom_call_target="tpu_custom_call" | custom-call | tf_op jit(solution)/shard_map/apply/pallas_call | solution.py:391
